TPU v7x, 8 devices: a whole 2x2x1 slice. The times are simulated.
8 devices in a mesh: dp: 1 (over z), sp: 8 (over y, x, core).
Axes of the slice: x: 2, y: 2, z: 1, core: 2. Of those that a mesh axis runs over, the one named last changes fastest.
Arguments:
- tokens: bfloat16 [16, 2048, 4096], P('dp', 'sp')
- w_query: bfloat16 [4096, 4096], replicated
- w_key: bfloat16 [4096, 1024], replicated
- w_value: bfloat16 [4096, 1024], replicated
- w_out: bfloat16 [4096, 4096], replicated
- attn_norm: bfloat16 [4096], replicated
- q_norm: bfloat16 [128], replicated
- k_norm: bfloat16 [128], replicated
Outputs:
- output 1: bfloat16 [16, 2048, 4096], P('dp', 'sp')
- output 2: bfloat16 [16, 2048, 8, 128], P('dp', 'sp')
- output 3: bfloat16 [16, 2048, 8, 128], P('dp', 'sp')
All inputs are finite; a program needn't handle non-finite values.
Results may differ from a plain program's by a relative error of at most 0.00828378.
Values are sent between devices in bfloat16 or wider.
A program may use at most 1 GiB of HBM per device.

v0:
```python
import jax
import jax.numpy as jnp
from jax import lax
from jax.sharding import PartitionSpec as P

EPS = 1e-6
THETA = 1000000.0
HEAD_DIM = 128


def rms_norm(values, gain_vec):
    wide_vals = values.astype(jnp.float32)
    inv_rms = lax.rsqrt(jnp.mean(wide_vals * wide_vals, axis=-1, keepdims=True) + EPS)
    return wide_vals * inv_rms * gain_vec.astype(jnp.float32)


def rope_rotate(values, positions):
    half_dim = HEAD_DIM // 2
    inv_freq = THETA ** (-jnp.arange(half_dim, dtype=jnp.float32) * 2.0 / HEAD_DIM)
    angles = positions.astype(jnp.float32)[:, None] * inv_freq[None, :]
    cos_t = jnp.cos(angles)[None, :, None, :]
    sin_t = jnp.sin(angles)[None, :, None, :]
    lo_half = values[..., :half_dim]
    hi_half = values[..., half_dim:]
    return jnp.concatenate([lo_half * cos_t - hi_half * sin_t, hi_half * cos_t + lo_half * sin_t], axis=-1)


def qkv_local(tokens, w_query, w_key, w_value, attn_norm, q_norm, k_norm, positions):
    n_batch, n_tok, d_model = tokens.shape
    hidden = rms_norm(tokens, attn_norm).astype(jnp.bfloat16).reshape(n_batch * n_tok, d_model)

    def project(weight):
        flat_out = jnp.dot(hidden, weight, preferred_element_type=jnp.float32).astype(jnp.bfloat16)
        return flat_out.reshape(n_batch, n_tok, weight.shape[1] // HEAD_DIM, HEAD_DIM)

    q_rot = rope_rotate(rms_norm(project(w_query), q_norm), positions).astype(jnp.bfloat16)
    k_rot = rope_rotate(rms_norm(project(w_key), k_norm), positions).astype(jnp.bfloat16)
    return q_rot, k_rot, project(w_value)


def finish_block(tokens, attn_heads, w_out):
    n_batch, n_tok, d_model = tokens.shape
    flat_in = attn_heads.reshape(n_batch * n_tok, w_out.shape[0])
    proj_out = jnp.dot(flat_in, w_out, preferred_element_type=jnp.float32).reshape(n_batch, n_tok, d_model)
    return (tokens.astype(jnp.float32) + proj_out).astype(jnp.bfloat16)


def causal_attention(q_group, k_seq, v_seq, q_offset):
    n_batch, q_len, n_kv, n_group, head_dim = q_group.shape
    blk_len = min(256, q_len)
    n_qblk = q_len // blk_len
    scale = head_dim ** -0.5
    q_blocks = q_group.reshape(n_batch, n_qblk, blk_len, n_kv, n_group, head_dim)
    row_ids = jnp.arange(blk_len)
    stat_shape = (n_batch, blk_len, n_kv, n_group)

    def one_block(blk_idx):
        q_blk = lax.dynamic_index_in_dim(q_blocks, blk_idx, axis=1, keepdims=False)
        q_start = q_offset + blk_idx * blk_len
        n_kblk = q_start // blk_len + 1

        def key_step(key_blk, carry):
            run_max, run_sum, out_acc = carry
            k_blk = lax.dynamic_slice_in_dim(k_seq, key_blk * blk_len, blk_len, axis=1)
            v_blk = lax.dynamic_slice_in_dim(v_seq, key_blk * blk_len, blk_len, axis=1)
            scores = jnp.einsum('bqkgd,bskd->bqkgs', q_blk, k_blk, preferred_element_type=jnp.float32) * scale
            allowed = (key_blk * blk_len + row_ids)[None, :] <= (q_start + row_ids)[:, None]
            scores = jnp.where(allowed[None, :, None, None, :], scores, -jnp.inf)
            new_max = jnp.maximum(run_max, jnp.max(scores, axis=-1))
            rescale = jnp.exp(run_max - new_max)
            probs_blk = jnp.exp(scores - new_max[..., None])
            run_sum = run_sum * rescale + jnp.sum(probs_blk, axis=-1)
            out_acc = out_acc * rescale[..., None] + jnp.einsum('bqkgs,bskd->bqkgd', probs_blk.astype(jnp.bfloat16), v_blk, preferred_element_type=jnp.float32)
            return new_max, run_sum, out_acc

        init_state = (jnp.full(stat_shape, -jnp.inf, jnp.float32), jnp.zeros(stat_shape, jnp.float32), jnp.zeros(stat_shape + (head_dim,), jnp.float32))
        final_state = lax.fori_loop(0, n_kblk, key_step, init_state)
        return (final_state[2] / final_state[1][..., None]).astype(jnp.bfloat16)

    attn_blocks = lax.map(one_block, jnp.arange(n_qblk))
    return jnp.moveaxis(attn_blocks, 0, 1).reshape(n_batch, q_len, n_kv, n_group, head_dim)


def solution(mesh):
    n_sp = mesh.shape['sp']

    def per_device(tokens, w_query, w_key, w_value, w_out, attn_norm, q_norm, k_norm):
        n_batch, seq_loc, d_model = tokens.shape
        positions = lax.axis_index('sp') * seq_loc + jnp.arange(seq_loc)
        q_rot, k_rot, v_proj = qkv_local(tokens, w_query, w_key, w_value, attn_norm, q_norm, k_norm, positions)
        n_kv = k_rot.shape[2]
        copies = max(1, n_sp // n_kv)
        k_send = jnp.repeat(k_rot, copies, axis=2) if copies > 1 else k_rot
        v_send = jnp.repeat(v_proj, copies, axis=2) if copies > 1 else v_proj
        q_heads = lax.all_to_all(q_rot, 'sp', 2, 1, tiled=True)
        k_heads = lax.all_to_all(k_send, 'sp', 2, 1, tiled=True)
        v_heads = lax.all_to_all(v_send, 'sp', 2, 1, tiled=True)
        seq_len = q_heads.shape[1]
        h_loc = q_heads.shape[2]
        kv_loc = k_heads.shape[2]
        attn_out = causal_attention(q_heads.reshape(n_batch, seq_len, kv_loc, h_loc // kv_loc, HEAD_DIM), k_heads, v_heads, 0)
        attn_seq = lax.all_to_all(attn_out.reshape(n_batch, seq_len, h_loc, HEAD_DIM), 'sp', 1, 2, tiled=True)
        return finish_block(tokens, attn_seq, w_out), k_rot, v_proj

    spec_tok = P('dp', 'sp', None)
    spec_cache = P('dp', 'sp', None, None)
    spec_mat = P(None, None)
    spec_vec = P(None)
    return jax.shard_map(per_device, mesh=mesh, in_specs=(spec_tok, spec_mat, spec_mat, spec_mat, spec_mat, spec_vec, spec_vec, spec_vec), out_specs=(spec_tok, spec_cache, spec_cache), check_vma=False)
```

profile of v0, /device:TPU:0, one launch (start us, length us, event | category | flops | bytes accessed | tf_op | source)
XLA Modules:
  0.0 3197.4 jit_solution(2446606044633654780)
XLA Ops:
  12.7 23.2 fusion.28
  35.8 42.2 %convert_bitcast_fusion.2 = bf16[512,8,8,128]{3,1,2,0:T(8,128)(2,1)} fusion(bf16[4096,4096]{1,0:T(8,128)(2,1)} %bitcast.149, bf16[4096,1024]{1,0:T(8,128)(2,1)} %param.15), kind=kOutput, calls=%fused_computation.56 | convolution fusion | flops 34363932672 | bytes 50331648 | tf_op jit(solution)/shard_map/dot_general | solution.py:33
  101.8 41.0 %convert_bitcast_fusion.1 = f32[512,8,8,128]{3,1,2,0:T(8,128)S(1)} fusion(bf16[4096,4096]{1,0:T(8,128)(2,1)} %bitcast.150, bf16[4096,1024]{1,0:T(8,128)(2,1)} %param.14), kind=kOutput, calls=%fused_computation.51 | convolution fusion | flops 34368126976 | bytes 58720256 | tf_op jit(solution)/shard_map/dot_general | solution.py:33
  158.4 151.2 %convert_bitcast_fusion = f32[512,8,32,128]{3,1,2,0:T(8,128)} fusion(bf16[4096,4096]{1,0:T(8,128)(2,1)} %bitcast.151, bf16[4096,4096]{1,0:T(8,128)(2,1)} %param.13), kind=kOutput, calls=%fused_computation.43 | convolution fusion | flops 137472507904 | bytes 134217728 | tf_op jit(solution)/shard_map/dot_general | solution.py:33
  309.6 44.1 %copy.61 = f32[512,8,32,128]{3,2,1,0:T(8,128)} copy(f32[512,8,32,128]{3,1,2,0:T(8,128)} %convert_bitcast_fusion) | data formatting | bytes 134217728
  353.7 22.1 multiply_reduce_fusion
  406.5 45.3 %fusion.30 = f32[16,256,32,128]{3,1,0,2:T(8,128)} fusion(f32[16,256,32,128]{3,2,1,0:T(8,128)} %bitcast.51, f32[128]{0:T(128)S(1)} %copy-done.3, f32[16,256,32]{1,0,2:T(8,128)S(1)} %copy.39), kind=kLoop, calls=%fused_computation.42 | loop fusion | flops 33554432 | bytes 134742528 | tf_op jit(solution)/shard_map/mul | solution.py:14
  451.8 66.1 %subtract_convert_fusion = (bf16[16,256,32,64]{3,1,0,2:T(8,128)(2,1)}, bf16[16,256,32,64]{3,1,0,2:T(8,128)(2,1)}) fusion(f32[16,256,32,128]{3,1,0,2:T(8,128)} %fusion.30, f32[256,64]{1,0:T(8,128)S(1)} %get-tuple-element.285, f32[256,64]{1,0:T(8,128)S(1)} %get-tuple-element.284), kind=kLoop, calls=%fused_computation.45 | loop fusion | flops 67108864 | bytes 100794368 | tf_op jit(solution)/shard_map/convert.4
  517.9 33.4 %pad_maximum_fusion = bf16[16,256,32,128]{3,1,0,2:T(8,128)(2,1)} fusion(bf16[16,256,32,64]{3,1,0,2:T(8,128)(2,1)} %get-tuple-element.281, bf16[16,256,32,64]{3,1,0,2:T(8,128)(2,1)} %get-tuple-element.280), kind=kLoop, calls=%fused_computation.47 | loop fusion | flops 67108864 | bytes 67108864 | tf_op jit(solution)/shard_map/concatenate | solution.py:25
  585.4 335.9 %all-to-all-done = bf16[16,256,32,128]{3,1,0,2:T(8,128)(2,1)} async-done(((bf16[16,256,32,128]{3,1,0,2:T(8,128)(2,1)}), bf16[16,256,32,128]{3,1,0,2:T(8,128)(2,1)}, u32[]{:S(2)}, u32[]{:S(2)}) %all-to-all-start) | async-done | bytes 33554464 | tf_op jit(solution)/shard_map/all_to_all | solution.py:95
  921.3 22.9 copy.41
  944.2 1570.5 %while.44 = (s32[]{:T(128)}, bf16[8,16,256,1,4,128]{5,2,0,4,1,3:T(8,128)(2,1)}, s32[8]{0:T(128)S(1)}, bf16[16,8,256,1,4,128]{5,2,4,1,0,3:T(8,128)(2,1)}, bf16[16...) while((s32[]{:T(128)}, ...), condition=%wide.region_8.9_spmd.clone.clone, body=%wide.region_3.8_spmd.clone.clone.sunk | while | flops 2202124800 | bytes 121051864 | solution.py:80
  956.4 36.8 %while.45 = (s32[]{:T(128)}, f32[16,256,1,4]{1,3,0,2:T(4,128)S(1)}, f32[16,256,1,4]{1,3,0,2:T(4,128)S(1)}, f32[16,256,1,4,128]{1,4,3,0,2:T(8,128)}, s32[]{:T(128...) while((s32[]{:T(128)}, f32[16,256,1,4]{1,3,0,2:T(4,128)S(1)}, ...), condition=%wide.region_7.7_spmd.clone, body=%wide.region_4.6_spmd.clone.sunk | while | flops 2197930496 | bytes 74716360 | solution.py:77
  1023.7 73.6 %while.45 = (s32[]{:T(128)}, f32[16,256,1,4]{1,3,0,2:T(4,128)S(1)}, f32[16,256,1,4]{1,3,0,2:T(4,128)S(1)}, f32[16,256,1,4,128]{1,4,3,0,2:T(8,128)}, s32[]{:T(128...) while((s32[]{:T(128)}, f32[16,256,1,4]{1,3,0,2:T(4,128)S(1)}, ...), condition=%wide.region_7.7_spmd.clone, body=%wide.region_4.6_spmd.clone.sunk | while | flops 2197930496 | bytes 74716360 | solution.py:77
  1127.9 110.5 %while.45 = (s32[]{:T(128)}, f32[16,256,1,4]{1,3,0,2:T(4,128)S(1)}, f32[16,256,1,4]{1,3,0,2:T(4,128)S(1)}, f32[16,256,1,4,128]{1,4,3,0,2:T(8,128)}, s32[]{:T(128...) while((s32[]{:T(128)}, f32[16,256,1,4]{1,3,0,2:T(4,128)S(1)}, ...), condition=%wide.region_7.7_spmd.clone, body=%wide.region_4.6_spmd.clone.sunk | while | flops 2197930496 | bytes 74716360 | solution.py:77
  1222.0 16.3 bitcast_add_fusion.5
  1268.9 147.3 %while.45 = (s32[]{:T(128)}, f32[16,256,1,4]{1,3,0,2:T(4,128)S(1)}, f32[16,256,1,4]{1,3,0,2:T(4,128)S(1)}, f32[16,256,1,4,128]{1,4,3,0,2:T(8,128)}, s32[]{:T(128...) while((s32[]{:T(128)}, f32[16,256,1,4]{1,3,0,2:T(4,128)S(1)}, ...), condition=%wide.region_7.7_spmd.clone, body=%wide.region_4.6_spmd.clone.sunk | while | flops 2197930496 | bytes 74716360 | solution.py:77
  1326.2 16.3 bitcast_add_fusion.5
  1399.9 16.3 bitcast_add_fusion.5
  1446.7 184.1 %while.45 = (s32[]{:T(128)}, f32[16,256,1,4]{1,3,0,2:T(4,128)S(1)}, f32[16,256,1,4]{1,3,0,2:T(4,128)S(1)}, f32[16,256,1,4,128]{1,4,3,0,2:T(8,128)}, s32[]{:T(128...) while((s32[]{:T(128)}, f32[16,256,1,4]{1,3,0,2:T(4,128)S(1)}, ...), condition=%wide.region_7.7_spmd.clone, body=%wide.region_4.6_spmd.clone.sunk | while | flops 2197930496 | bytes 74716360 | solution.py:77
  1661.4 221.0 %while.45 = (s32[]{:T(128)}, f32[16,256,1,4]{1,3,0,2:T(4,128)S(1)}, f32[16,256,1,4]{1,3,0,2:T(4,128)S(1)}, f32[16,256,1,4,128]{1,4,3,0,2:T(8,128)}, s32[]{:T(128...) while((s32[]{:T(128)}, f32[16,256,1,4]{1,3,0,2:T(4,128)S(1)}, ...), condition=%wide.region_7.7_spmd.clone, body=%wide.region_4.6_spmd.clone.sunk | while | flops 2197930496 | bytes 74716360 | solution.py:77
  1866.0 16.3 bitcast_add_fusion.5
  1912.9 257.8 %while.45 = (s32[]{:T(128)}, f32[16,256,1,4]{1,3,0,2:T(4,128)S(1)}, f32[16,256,1,4]{1,3,0,2:T(4,128)S(1)}, f32[16,256,1,4,128]{1,4,3,0,2:T(8,128)}, s32[]{:T(128...) while((s32[]{:T(128)}, f32[16,256,1,4]{1,3,0,2:T(4,128)S(1)}, ...), condition=%wide.region_7.7_spmd.clone, body=%wide.region_4.6_spmd.clone.sunk | while | flops 2197930496 | bytes 74716360 | solution.py:77
  2117.6 16.3 bitcast_add_fusion.5
  2201.3 294.7 %while.45 = (s32[]{:T(128)}, f32[16,256,1,4]{1,3,0,2:T(4,128)S(1)}, f32[16,256,1,4]{1,3,0,2:T(4,128)S(1)}, f32[16,256,1,4,128]{1,4,3,0,2:T(8,128)}, s32[]{:T(128...) while((s32[]{:T(128)}, f32[16,256,1,4]{1,3,0,2:T(4,128)S(1)}, ...), condition=%wide.region_7.7_spmd.clone, body=%wide.region_4.6_spmd.clone.sunk | while | flops 2197930496 | bytes 74716360 | solution.py:77
  2405.9 16.3 bitcast_add_fusion.5
  2514.7 42.1 %copy.51 = bf16[16,2048,4,128]{3,2,0,1:T(4,128)(2,1)} copy(bf16[16,2048,4,128]{3,1,2,0:T(8,128)(2,1)} %bitcast.145) | data formatting | bytes 67108864 | tf_op jit(solution)/shard_map/reshape;reshape | solution.py:102
  2576.4 350.0 %all-to-all-done.3 = bf16[16,2048,4,128]{3,2,0,1:T(4,128)(2,1)} async-done(((bf16[16,2048,4,128]{3,2,0,1:T(4,128)(2,1)}), bf16[16,2048,4,128]{3,2,0,1:T(4,128)(2,1)}, u32[]{:S(2)}, u32[]{:S(2)}) %all-to-all-start.3) | async-done | bytes 33554464 | tf_op jit(solution)/shard_map/all_to_all | solution.py:102
  2926.5 23.3 copy.52
  2949.8 42.2 %copy.53 = bf16[16,256,8,4,128]{4,3,2,1,0:T(4,128)(2,1)} copy(bf16[16,256,8,4,128]{4,1,2,3,0:T(8,128)(2,1)} %bitcast.142) | data formatting | bytes 67108864 | tf_op jit(solution)/shard_map/all_to_all | solution.py:102
  2992.0 54.3 %dot_general.25 = bf16[16,256,4096]{2,1,0:T(8,128)(2,1)} reshape(bf16[16,256,8,4,128]{4,3,2,1,0:T(4,128)(2,1)} %copy.53) | data formatting | bytes 67108864 | tf_op jit(solution)/shard_map/dot_general | solution.py:44
  3046.3 150.7 %fusion.29 = bf16[16,256,4096]{2,1,0:T(8,128)(2,1)} fusion(bf16[16,256,4096]{2,1,0:T(8,128)(2,1)} %param.12, bf16[16,256,4096]{2,1,0:T(8,128)(2,1)} %dot_general.25, bf16[4096,4096]{1,0:T(8,128)(2,1)} %param.16), kind=kOutput, calls=%fused_computation.40 | convolution fusion | flops 137489285120 | bytes 134217728 | tf_op jit(solution)/shard_map/dot_general | solution.py:44
  (399 shorter events, 1586.2 us)
Async XLA Ops:
  87.0 13.7 copy-start.4
  87.0 14.3 copy-start.5
  95.8 307.0 %all-to-all-start.2 = ((bf16[16,256,8,128]{3,1,0,2:T(8,128)(2,1)}), bf16[16,256,8,128]{3,1,0,2:T(8,128)(2,1)}, u32[]{:S(2)}, u32[]{:S(2)}) async-start(bf16[16,256,8,128]{3,1,0,2:T(8,128)(2,1)} %copy.46), calls=%async_computation.2 | async-start | bytes 16777216 | tf_op jit(solution)/shard_map/all_to_all | solution.py:97
  146.6 5.7 copy-start
  353.7 23.7 copy-start.1
  353.7 23.7 copy-start.2
  393.4 13.1 copy-start.3
  402.8 148.5 %all-to-all-start.1 = ((bf16[16,256,8,128]{3,1,0,2:T(8,128)(2,1)}), bf16[16,256,8,128]{3,1,0,2:T(8,128)(2,1)}, u32[]{:S(2)}, u32[]{:S(2)}) async-start(bf16[16,256,8,128]{3,1,0,2:T(8,128)(2,1)} %pad_maximum_fusion.1), calls=%async_computation.1 | async-start | bytes 16777216 | tf_op jit(solution)/shard_map/all_to_all | solution.py:96
  551.3 370.0 %all-to-all-start = ((bf16[16,256,32,128]{3,1,0,2:T(8,128)(2,1)}), bf16[16,256,32,128]{3,1,0,2:T(8,128)(2,1)}, u32[]{:S(2)}, u32[]{:S(2)}) async-start(bf16[16,256,32,128]{3,1,0,2:T(8,128)(2,1)} %pad_maximum_fusion), calls=%async_computation | async-start | bytes 67108864 | tf_op jit(solution)/shard_map/all_to_all | solution.py:95
  2556.8 369.7 %all-to-all-start.3 = ((bf16[16,2048,4,128]{3,2,0,1:T(4,128)(2,1)}), bf16[16,2048,4,128]{3,2,0,1:T(4,128)(2,1)}, u32[]{:S(2)}, u32[]{:S(2)}) async-start(bf16[16,2048,4,128]{3,2,0,1:T(4,128)(2,1)} %copy.51), calls=%async_computation.3 | async-start | bytes 67108864 | tf_op jit(solution)/shard_map/all_to_all | solution.py:102
where the time goes:
time: 3210 us; the launch traced here: 3200 us
  matrix products  1350 us (42%)
  waiting for transfers between devices  686 us (21%)
  other arithmetic  643 us (20%)
  local copies, waits for them, and re-layouts  472 us (15%)
    dot_general x36, matrix products, key_step(): jnp.einsum('bqkgs,bskd->bqkgd', probs_blk.astype(jnp.bfloat16), v_blk, pr...  585 us
    dot_general x36, matrix products, key_step(): jnp.einsum('bqkgd,bskd->bqkgs', q_blk, k_blk, preferred_element_type=jnp....  382 us
    all_to_all x1, waiting for transfers between devices, per_device(): lax.all_to_all(attn_out.reshape(n_batch, seq_len, h_loc, HEAD_DIM), 'sp',...  350 us
    reduce_sum x36, other arithmetic, key_step(): run_sum = run_sum * rescale + jnp.sum(probs_blk, axis=-1)  349 us
    all_to_all x1, waiting for transfers between devices, per_device(): q_heads = lax.all_to_all(q_rot, 'sp', 2, 1, tiled=True)  336 us
    dot_general x3, matrix products, project(): jnp.dot(hidden, weight, preferred_element_type=jnp.float32)  234 us
    dot_general x1, matrix products, finish_block(): jnp.dot(flat_in, w_out, preferred_element_type=jnp.float32)  151 us
    dynamic_update_slice x16, local copies, waits for them, and re-layouts, causal_attention(): attn_blocks = lax.map(one_block, jnp.arange(n_qblk))  95.3 us
  transfers between devices with their start and end apart: 4, of which 2 were waited for; matrix products, arithmetic and copies ran while one was open for 15% of the time, Pallas kernels for 0%

commit v1 on v0

v1 whole, which is shorter than its diff:
```python
import functools

import jax
import jax.numpy as jnp
from jax import lax
from jax.experimental import pallas as pl
from jax.experimental.pallas import tpu as pltpu
from jax.sharding import PartitionSpec as P

EPS = 1e-6
THETA = 1000000.0
HD = 128
LOG2E = 1.4426950408889634
VMEM_LIMIT = 60 * 1024 * 1024


def rope_tables(positions):
    half = HD // 2
    inv_freq = THETA ** (-jnp.arange(half, dtype=jnp.float32) * 2.0 / HD)
    angles = positions.astype(jnp.float32)[:, None] * inv_freq[None, :]
    cos_t, sin_t = jnp.cos(angles), jnp.sin(angles)
    return jnp.concatenate([cos_t, cos_t], axis=1), jnp.concatenate([-sin_t, sin_t], axis=1)


def head_norm_rope(raw, gain, cos_t, sin_t):
    inv = lax.rsqrt(jnp.mean(raw * raw, axis=-1, keepdims=True) + EPS)
    normed = raw * inv * gain
    return normed * cos_t + pltpu.roll(normed, HD // 2, 1) * sin_t


def kv_kernel(x_ref, g_ref, wk_ref, wv_ref, kg_ref, cos_ref, sin_ref, h_ref, kv_ref):
    wide = x_ref[...].astype(jnp.float32)
    inv = lax.rsqrt(jnp.mean(wide * wide, axis=-1, keepdims=True) + EPS)
    h_ref[...] = (wide * inv * g_ref[...]).astype(jnp.bfloat16)
    hid = h_ref[...]
    n_k = wk_ref.shape[1]
    step = 512
    for c in range(0, n_k, step):
        raw = jnp.dot(hid, wk_ref[:, c:c + step], preferred_element_type=jnp.float32)
        raw = raw.astype(jnp.bfloat16).astype(jnp.float32)
        for j in range(0, step, HD):
            k_rot = head_norm_rope(raw[:, j:j + HD], kg_ref[...], cos_ref[...], sin_ref[...])
            kv_ref[:, c + j:c + j + HD] = k_rot.astype(jnp.bfloat16)
    for c in range(0, n_k, step):
        raw = jnp.dot(hid, wv_ref[:, c:c + step], preferred_element_type=jnp.float32)
        kv_ref[:, n_k + c:n_k + c + step] = raw.astype(jnp.bfloat16)


def kv_project(x, w_key, w_value, attn_gain, k_gain, cos_t, sin_t):
    rows, d_model = x.shape
    n_k = w_key.shape[1]
    tok = cos_t.shape[0]
    bm = 256
    rep = tok // bm
    tab = pl.BlockSpec((bm, HD), lambda i: (i % rep, 0))
    full = lambda a: pl.BlockSpec(a.shape, lambda i: (0, 0), pipeline_mode=pl.Buffered(1))
    return pl.pallas_call(
        kv_kernel,
        grid=(rows // bm,),
        in_specs=[pl.BlockSpec((bm, d_model), lambda i: (i, 0)), full(attn_gain), full(w_key), full(w_value), full(k_gain), tab, tab],
        out_specs=[pl.BlockSpec((bm, d_model), lambda i: (i, 0)), pl.BlockSpec((bm, 2 * n_k), lambda i: (i, 0))],
        out_shape=[jax.ShapeDtypeStruct((rows, d_model), jnp.bfloat16), jax.ShapeDtypeStruct((rows, 2 * n_k), jnp.bfloat16)],
        compiler_params=pltpu.CompilerParams(vmem_limit_bytes=VMEM_LIMIT, dimension_semantics=('arbitrary',)),
        cost_estimate=pl.CostEstimate(flops=2 * rows * d_model * 2 * n_k, bytes_accessed=rows * d_model * 4 + 4 * d_model * n_k, transcendentals=0),
        name='kv_project',
    )(x, attn_gain, w_key, w_value, k_gain, cos_t, sin_t)


def attn_kernel(n_group, blk, idx_ref, q_ref, k_ref, v_ref, qg_ref, cos_ref, sin_ref, o_ref, q_s, acc_s, m_s, l_s):
    idx = idx_ref[0]
    scale = LOG2E * HD ** -0.5
    for h in range(n_group):
        raw = q_ref[:, h * HD:(h + 1) * HD].astype(jnp.float32)
        q_s[h] = head_norm_rope(raw, qg_ref[...], cos_ref[...], sin_ref[...]).astype(jnp.bfloat16)

    def fold(p):
        part = p[:, :HD]
        for j in range(HD, p.shape[1], HD):
            part = part + p[:, j:j + HD]
        return part

    def scores(h, k_blk):
        return lax.dot_general(q_s[h], k_blk, (((1,), (1,)), ((), ())), preferred_element_type=jnp.float32) * scale

    def first(start, n_blk):
        k_blk = k_ref[pl.ds(start, n_blk)].reshape(n_blk * blk, HD)
        v_blk = v_ref[pl.ds(start, n_blk)].reshape(n_blk * blk, HD)
        shape = (blk, n_blk * blk)
        allowed = lax.broadcasted_iota(jnp.int32, shape, 1) <= lax.broadcasted_iota(jnp.int32, shape, 0) + (n_blk - 1) * blk
        for h in range(n_group):
            s = jnp.where(allowed, scores(h, k_blk), -jnp.inf)
            m = jnp.broadcast_to(jnp.max(s, axis=1, keepdims=True), (blk, HD))
            p = jnp.exp2(s - jnp.concatenate([m] * (shape[1] // HD), axis=1))
            m_s[h] = m
            l_s[h] = fold(p)
            acc_s[h] = jnp.dot(p.astype(jnp.bfloat16), v_blk, preferred_element_type=jnp.float32)

    pl.when(idx % 2 == 0)(lambda: first(idx, 1))
    pl.when(idx % 2 == 1)(lambda: first(idx - 1, 2))

    def body(j, _):
        k_blk = k_ref[pl.ds(2 * j, 2)].reshape(2 * blk, HD)
        v_blk = v_ref[pl.ds(2 * j, 2)].reshape(2 * blk, HD)
        for h in range(n_group):
            s = scores(h, k_blk)
            m_old = m_s[h]
            m = jnp.maximum(m_old, jnp.broadcast_to(jnp.max(s, axis=1, keepdims=True), (blk, HD)))
            alpha = jnp.exp2(m_old - m)
            p = jnp.exp2(s - jnp.concatenate([m] * (2 * blk // HD), axis=1))
            m_s[h] = m
            l_s[h] = l_s[h] * alpha + fold(p)
            acc_s[h] = acc_s[h] * alpha + jnp.dot(p.astype(jnp.bfloat16), v_blk, preferred_element_type=jnp.float32)
        return 0

    lax.fori_loop(0, idx // 2, body, 0)
    for h in range(n_group):
        total = jnp.sum(l_s[h], axis=1, keepdims=True)
        o_ref[:, h * HD:(h + 1) * HD] = (acc_s[h] * (1.0 / total)).astype(jnp.bfloat16)


def attention(idx, q, kv_all, q_gain, cos_t, sin_t):
    n_dev, rows, kv_w = kv_all.shape
    n_kv = kv_w // (2 * HD)
    n_group = q.shape[1] // (n_kv * HD)
    blk = cos_t.shape[0]
    n_b = rows // blk
    tab = pl.BlockSpec((blk, HD), lambda b, h, i: (0, 0))
    qo = pl.BlockSpec((blk, n_group * HD), lambda b, h, i: (b, h))
    flops = 4 * rows * q.shape[1] * n_dev * blk * 2
    return pl.pallas_call(
        functools.partial(attn_kernel, n_group, blk),
        grid_spec=pltpu.PrefetchScalarGridSpec(
            num_scalar_prefetch=1,
            grid=(n_b, n_kv),
            in_specs=[qo, pl.BlockSpec((n_dev, blk, HD), lambda b, h, i: (0, b, h)), pl.BlockSpec((n_dev, blk, HD), lambda b, h, i: (0, b, n_kv + h)), pl.BlockSpec((1, HD), lambda b, h, i: (0, 0)), tab, tab],
            out_specs=qo,
            scratch_shapes=[pltpu.VMEM((n_group, blk, HD), jnp.bfloat16)] + [pltpu.VMEM((n_group, blk, HD), jnp.float32)] * 3,
        ),
        out_shape=jax.ShapeDtypeStruct(q.shape, jnp.bfloat16),
        compiler_params=pltpu.CompilerParams(vmem_limit_bytes=VMEM_LIMIT, dimension_semantics=('arbitrary', 'arbitrary')),
        cost_estimate=pl.CostEstimate(flops=flops, bytes_accessed=4 * rows * q.shape[1] + 2 * kv_all.size, transcendentals=0),
        name='attention',
    )(idx, q, kv_all, kv_all, q_gain, cos_t, sin_t)


def solution(mesh):
    def per_device(tokens, w_query, w_key, w_value, w_out, attn_norm, q_norm, k_norm):
        n_batch, seq_loc, d_model = tokens.shape
        me = lax.axis_index('sp')
        cos_t, sin_t = rope_tables(me * seq_loc + jnp.arange(seq_loc))
        attn_gain = attn_norm.astype(jnp.float32)[None, :]
        q_gain = q_norm.astype(jnp.float32)[None, :]
        k_gain = k_norm.astype(jnp.float32)[None, :]
        idx = jnp.reshape(me, (1,)).astype(jnp.int32)
        flat = tokens.reshape(n_batch * seq_loc, d_model)
        n_kv = w_key.shape[1] // HD

        n_chunk = 4
        rows = n_batch * seq_loc // n_chunk
        parts = [flat[g * rows:(g + 1) * rows] for g in range(n_chunk)]
        hid, kv, kv_all = [], [], []
        for g in range(n_chunk):
            h_g, kv_g = kv_project(parts[g], w_key, w_value, attn_gain, k_gain, cos_t, sin_t)
            hid.append(h_g)
            kv.append(kv_g)
            kv_all.append(lax.all_gather(kv_g, 'sp', axis=0, tiled=False))
        outs = []
        for g in range(n_chunk):
            q_g = jnp.dot(hid[g], w_query, preferred_element_type=jnp.float32).astype(jnp.bfloat16)
            o_g = attention(idx, q_g, kv_all[g], q_gain, cos_t, sin_t)
            proj = jnp.dot(o_g, w_out, preferred_element_type=jnp.float32)
            outs.append((parts[g].astype(jnp.float32) + proj).astype(jnp.bfloat16))
        out = jnp.concatenate(outs, axis=0).reshape(tokens.shape)
        kv_cat = jnp.concatenate(kv, axis=0)
        k_cache = kv_cat[:, :n_kv * HD].reshape(n_batch, seq_loc, n_kv, HD)
        v_cache = kv_cat[:, n_kv * HD:].reshape(n_batch, seq_loc, n_kv, HD)
        return out, k_cache, v_cache

    spec_tok = P('dp', 'sp', None)
    spec_cache = P('dp', 'sp', None, None)
    spec_mat = P(None, None)
    spec_vec = P(None)
    return jax.shard_map(per_device, mesh=mesh, in_specs=(spec_tok, spec_mat, spec_mat, spec_mat, spec_mat, spec_vec, spec_vec, spec_vec), out_specs=(spec_tok, spec_cache, spec_cache), check_vma=False)
```

time: 3210 us -> 1400 us (0.44)
  the two profiles are of different devices: /device:TPU:0 before, /device:TPU:7 now
where the time goes in v1:
time: 1400 us
  Pallas kernels  961 us (69%)
  matrix products  335 us (24%)
  local copies, waits for them, and re-layouts  58.6 us (4%)
  other arithmetic  27.4 us (2%)
  between operations  14.4 us (1%)
    pallas_call x4, Pallas kernels, attention(): pl.pallas_call(functools.partial(attn_kernel, n_group, blk), grid_spec=pl...  845 us
    dot_general x4, matrix products, per_device(): jnp.dot(hid[g], w_query, preferred_element_type=jnp.float32)  168 us
    dot_general x4, matrix products, per_device(): proj = jnp.dot(o_g, w_out, preferred_element_type=jnp.float32)  167 us
    pallas_call x4, Pallas kernels, kv_project(): pl.pallas_call(kv_kernel, grid=(rows // bm,), in_specs=[pl.BlockSpec((bm,...  116 us
    unnamed x24, local copies, waits for them, and re-layouts  35.3 us
  transfers between devices with their start and end apart: 4, of which 0 were waited for; matrix products, arithmetic and copies ran while one was open for 23% of the time, Pallas kernels for 52%

profile of v1, /device:TPU:7, one launch (start us, length us, event | category | flops | bytes accessed | tf_op | source)
XLA Modules:
  0.0 1396.2 jit_solution(3252653423302243232)
XLA Ops:
  7.2 1.2 bitcast_convert_fusion.1.kg_ref
  8.4 1.3 broadcast_in_dim.23
  9.7 23.0 %fusion.1 = (bf16[4,256,4096]{2,1,0:T(8,128)(2,1)}, bf16[4,256,4096]{2,1,0:T(8,128)(2,1)}, bf16[4,256,4096]{2,1,0:T(8,128)(2,1)}, bf16[4,256,4096]{2,1,0:T(8,128)(2,1)}) fusion(bf16[16,256,4096]{2,1,0:T(8,128)(2,1)} %param.8), kind=kLoop, calls=%fused_computation.24 | loop fusion | bytes 67108864 | tf_op jit(solution)/shard_map/slice | solution.py:160
  32.7 0.5 fusion
  33.2 0.8 pad_maximum_fusion.1
  34.1 28.9 %kv_project.5 = (bf16[1024,4096]{1,0:T(8,128)(2,1)}, bf16[1024,2048]{1,0:T(8,128)(2,1)}) custom-call(bf16[1024,4096]{1,0:T(8,128)(2,1)} %bitcast.50, f32[1,4096]{1,0:T(1,128)} %bitcast.52, bf16[4096,1024]{1,0:T(8,128)(2,1)} %wk_ref.7, bf16[4096,1024]{1,0:T(8,128)(2,1)} %wv_ref.7, f32[1,128]{1,0:T(1,128)} %bitcast_convert_fusion.1.kg_ref, ...), custom_call_target="tpu_custom_call" | custom-call | flops 17179869184 | bytes 33554432 | tf_op jit(solution)/shard_map/kv_project/pallas_call | solution.py:57
  63.1 29.0 %kv_project.4 = (bf16[1024,4096]{1,0:T(8,128)(2,1)}, bf16[1024,2048]{1,0:T(8,128)(2,1)}) custom-call(bf16[1024,4096]{1,0:T(8,128)(2,1)} %bitcast.48, f32[1,4096]{1,0:T(1,128)} %bitcast.53, bf16[4096,1024]{1,0:T(8,128)(2,1)} %wk_ref.7, bf16[4096,1024]{1,0:T(8,128)(2,1)} %wv_ref.7, f32[1,128]{1,0:T(1,128)} %bitcast_convert_fusion.1.kg_ref, ...), custom_call_target="tpu_custom_call" | custom-call | flops 17179869184 | bytes 33554432 | tf_op jit(solution)/shard_map/kv_project/pallas_call | solution.py:57
  92.3 29.0 %kv_project.7 = (bf16[1024,4096]{1,0:T(8,128)(2,1)}, bf16[1024,2048]{1,0:T(8,128)(2,1)}) custom-call(bf16[1024,4096]{1,0:T(8,128)(2,1)} %bitcast.46, f32[1,4096]{1,0:T(1,128)} %bitcast.54, bf16[4096,1024]{1,0:T(8,128)(2,1)} %wk_ref.7, bf16[4096,1024]{1,0:T(8,128)(2,1)} %wv_ref.7, f32[1,128]{1,0:T(1,128)} %bitcast_convert_fusion.1.kg_ref, ...), custom_call_target="tpu_custom_call" | custom-call | flops 17179869184 | bytes 33554432 | tf_op jit(solution)/shard_map/kv_project/pallas_call | solution.py:57
  121.4 29.0 %kv_project.6 = (bf16[1024,4096]{1,0:T(8,128)(2,1)}, bf16[1024,2048]{1,0:T(8,128)(2,1)}) custom-call(bf16[1024,4096]{1,0:T(8,128)(2,1)} %bitcast.44, f32[1,4096]{1,0:T(1,128)} %bitcast.55, bf16[4096,1024]{1,0:T(8,128)(2,1)} %wk_ref.7, bf16[4096,1024]{1,0:T(8,128)(2,1)} %wv_ref.7, f32[1,128]{1,0:T(1,128)} %bitcast_convert_fusion.1.kg_ref, ...), custom_call_target="tpu_custom_call" | custom-call | flops 17179869184 | bytes 33554432 | tf_op jit(solution)/shard_map/kv_project/pallas_call | solution.py:57
  150.4 4.8 constant_dynamic-update-slice_fusion.3
  155.2 0.6 bitcast_convert_fusion.qg_ref
  155.8 42.4 %convolution_convert_fusion.2.q_ref = bf16[1024,4096]{1,0:T(8,128)(2,1)} fusion(bf16[1024,4096]{1,0:T(8,128)(2,1)} %get-tuple-element.13, bf16[4096,4096]{1,0:T(8,128)(2,1)} %param.9), kind=kOutput, calls=%fused_computation.9 | convolution fusion | flops 34363932672 | bytes 50331648 | tf_op jit(solution)/shard_map/dot_general | solution.py:169
  198.1 42.8 %convolution_convert_fusion.3.q_ref = bf16[1024,4096]{1,0:T(8,128)(2,1)} fusion(bf16[1024,4096]{1,0:T(8,128)(2,1)} %get-tuple-element.11, bf16[4096,4096]{1,0:T(8,128)(2,1)} %param.9), kind=kOutput, calls=%fused_computation.10 | convolution fusion | flops 34363932672 | bytes 50331648 | tf_op jit(solution)/shard_map/dot_general | solution.py:169
  240.9 2.7 constant_dynamic-update-slice_fusion.2
  243.6 0.8 copy-done.1
  244.4 0.3 constant_dynamic-update-slice_fusion.1
  244.7 0.9 copy-done.2
  245.6 0.3 constant_dynamic-update-slice_fusion
  245.9 7.7 slice_bitcast_fusion
  253.6 8.9 copy.12
  262.6 9.1 copy.11
  271.7 42.5 %convolution_convert_fusion.q_ref = bf16[1024,4096]{1,0:T(8,128)(2,1)} fusion(bf16[1024,4096]{1,0:T(8,128)(2,1)} %get-tuple-element.17, bf16[4096,4096]{1,0:T(8,128)(2,1)} %param.9), kind=kOutput, calls=%fused_computation.7 | convolution fusion | flops 34363932672 | bytes 50331648 | tf_op jit(solution)/shard_map/dot_general | solution.py:169
  314.2 40.4 %convolution_convert_fusion.1.q_ref = bf16[1024,4096]{1,0:T(8,128)(2,1)} fusion(bf16[1024,4096]{1,0:T(8,128)(2,1)S(1)} %bitcast.65, bf16[4096,4096]{1,0:T(8,128)(2,1)} %param.9), kind=kOutput, calls=%fused_computation.8 | convolution fusion | flops 34363932672 | bytes 50331648 | tf_op jit(solution)/shard_map/dot_general | solution.py:169
  354.6 211.1 %attention.5 = bf16[1024,4096]{1,0:T(8,128)(2,1)} custom-call(s32[1]{0:T(128)} %bitcast.1.idx_ref, bf16[1024,4096]{1,0:T(8,128)(2,1)} %convolution_convert_fusion.2.q_ref, bf16[8,1024,2048]{2,1,0:T(8,128)(2,1)} %bitcast.56, bf16[8,1024,2048]{2,1,0:T(8,128)(2,1)} %bitcast.57, f32[1,128]{1,0:T(1,128)} %bitcast_convert_fusion.qg_ref, ...), custom_call_target="tpu_custom_call" | custom-call | flops 68719476736 | bytes 50331648 | tf_op jit(solution)/shard_map/attention/pallas_call | solution.py:130
  565.7 211.3 %attention.4 = bf16[1024,4096]{1,0:T(8,128)(2,1)} custom-call(s32[1]{0:T(128)} %bitcast.1.idx_ref, bf16[1024,4096]{1,0:T(8,128)(2,1)} %convolution_convert_fusion.3.q_ref, bf16[8,1024,2048]{2,1,0:T(8,128)(2,1)} %bitcast.58, bf16[8,1024,2048]{2,1,0:T(8,128)(2,1)} %bitcast.59, f32[1,128]{1,0:T(1,128)} %bitcast_convert_fusion.qg_ref, ...), custom_call_target="tpu_custom_call" | custom-call | flops 68719476736 | bytes 50331648 | tf_op jit(solution)/shard_map/attention/pallas_call | solution.py:130
  777.0 211.1 %attention.7 = bf16[1024,4096]{1,0:T(8,128)(2,1)} custom-call(s32[1]{0:T(128)} %bitcast.1.idx_ref, bf16[1024,4096]{1,0:T(8,128)(2,1)} %convolution_convert_fusion.q_ref, bf16[8,1024,2048]{2,1,0:T(8,128)(2,1)} %bitcast.62, bf16[8,1024,2048]{2,1,0:T(8,128)(2,1)} %bitcast.63, f32[1,128]{1,0:T(1,128)} %bitcast_convert_fusion.qg_ref, ...), custom_call_target="tpu_custom_call" | custom-call | flops 68719476736 | bytes 50331648 | tf_op jit(solution)/shard_map/attention/pallas_call | solution.py:130
  988.1 42.2 %add_convert_fusion.2 = bf16[1024,4096]{1,0:T(8,128)(2,1)} fusion(bf16[1024,4096]{1,0:T(8,128)(2,1)} %bitcast.51, bf16[1024,4096]{1,0:T(8,128)(2,1)} %attention.5, bf16[4096,4096]{1,0:T(8,128)(2,1)} %param.12), kind=kOutput, calls=%fused_computation.3 | convolution fusion | flops 34372321280 | bytes 58720256 | tf_op jit(solution)/shard_map/dot_general | solution.py:171
  1030.3 40.7 %add_convert_fusion.3 = bf16[1024,4096]{1,0:T(8,128)(2,1)} fusion(bf16[1024,4096]{1,0:T(8,128)(2,1)S(1)} %bitcast.49, bf16[1024,4096]{1,0:T(8,128)(2,1)S(1)} %copy-done.6, bf16[4096,4096]{1,0:T(8,128)(2,1)} %param.12), kind=kOutput, calls=%fused_computation.4 | convolution fusion | flops 34372321280 | bytes 58720256 | tf_op jit(solution)/shard_map/dot_general | solution.py:171
  1071.0 41.7 %add_convert_fusion = bf16[1024,4096]{1,0:T(8,128)(2,1)} fusion(bf16[1024,4096]{1,0:T(8,128)(2,1)S(1)} %bitcast.47, bf16[1024,4096]{1,0:T(8,128)(2,1)} %attention.7, bf16[4096,4096]{1,0:T(8,128)(2,1)} %param.12), kind=kOutput, calls=%fused_computation.1 | convolution fusion | flops 34372321280 | bytes 58720256 | tf_op jit(solution)/shard_map/dot_general | solution.py:171
  1112.8 211.3 %attention.6 = bf16[1024,4096]{1,0:T(8,128)(2,1)} custom-call(s32[1]{0:T(128)} %bitcast.1.idx_ref, bf16[1024,4096]{1,0:T(8,128)(2,1)} %convolution_convert_fusion.1.q_ref, bf16[8,1024,2048]{2,1,0:T(8,128)(2,1)} %bitcast.60, bf16[8,1024,2048]{2,1,0:T(8,128)(2,1)} %bitcast.61, f32[1,128]{1,0:T(1,128)} %bitcast_convert_fusion.qg_ref, ...), custom_call_target="tpu_custom_call" | custom-call | flops 68719476736 | bytes 50331648 | tf_op jit(solution)/shard_map/attention/pallas_call | solution.py:130
  1324.1 42.1 %add_convert_fusion.1 = bf16[1024,4096]{1,0:T(8,128)(2,1)} fusion(bf16[1024,4096]{1,0:T(8,128)(2,1)} %bitcast.45, bf16[1024,4096]{1,0:T(8,128)(2,1)} %attention.6, bf16[4096,4096]{1,0:T(8,128)(2,1)} %param.12), kind=kOutput, calls=%fused_computation.2 | convolution fusion | flops 34372321280 | bytes 58720256 | tf_op jit(solution)/shard_map/dot_general | solution.py:171
  1366.2 23.0 %pad_maximum_fusion = bf16[4096,4096]{1,0:T(8,128)(2,1)} fusion(bf16[1024,4096]{1,0:T(8,128)(2,1)} %add_convert_fusion, bf16[1024,4096]{1,0:T(8,128)(2,1)} %add_convert_fusion.1, bf16[1024,4096]{1,0:T(8,128)(2,1)} %add_convert_fusion.2, bf16[1024,4096]{1,0:T(8,128)(2,1)} %add_convert_fusion.3), kind=kLoop, calls=%fused_computation | loop fusion | flops 134217728 | bytes 67108864 | tf_op jit(solution)/shard_map/concatenate | solution.py:173
  (31 shorter events, 0.5 us)
Async XLA Ops:
  7.2 347.5 %all-gather.11.cloned.1.call-start = ((), (), s32[]{:S(2)}) async-start(), calls=%async_computation.1 | async-start | bytes 37748736 | tf_op jit(solution)/shard_map/all_gather | solution.py:166
  63.0 502.7 %all-gather.9.cloned.1.call-start = ((), (), s32[]{:S(2)}) async-start(), calls=%async_computation | async-start | bytes 37748736 | tf_op jit(solution)/shard_map/all_gather | solution.py:166
  92.1 684.9 %all-gather.15.cloned.1.call-start = ((), (), s32[]{:S(2)}) async-start(), calls=%async_computation.3 | async-start | bytes 37748736 | tf_op jit(solution)/shard_map/all_gather | solution.py:166
  121.4 991.4 %all-gather.13.cloned.1.call-start = ((), (), s32[]{:S(2)}) async-start(), calls=%async_computation.2 | async-start | bytes 37748736 | tf_op jit(solution)/shard_map/all_gather | solution.py:166
  150.4 4.8 copy-start.5
  198.1 42.8 %copy-start = (bf16[4096,2048]{1,0:T(8,128)(2,1)S(1)}, bf16[4096,2048]{1,0:T(8,128)(2,1)}, u32[]{:S(2)}) copy-start(bf16[4096,2048]{1,0:T(8,128)(2,1)} %constant_dynamic-update-slice_fusion.3) | copy-start | bytes 50331652
  240.9 3.4 copy-start.1
  240.9 4.7 copy-start.2
  262.6 51.6 %slice-start = ((s8[8388608]{0:T(1024)(128)(4,1)}), s8[4194304]{0:T(1024)(128)(4,1)S(1)}, s32[]{:S(2)}) async-start(s8[8388608]{0:T(1024)(128)(4,1)} %bitcast.64), calls=%async_computation.4 | async-start | bytes 8388608
  271.7 42.5 %slice-start.1 = ((s8[8388608]{0:T(1024)(128)(4,1)}), s8[4194304]{0:T(1024)(128)(4,1)S(1)}, s32[]{:S(2)}) async-start(s8[8388608]{0:T(1024)(128)(4,1)} %bitcast.64), calls=%async_computation.5 | async-start | bytes 8388608
  988.1 42.2 %copy-start.4 = (bf16[4,256,4096]{2,1,0:T(8,128)(2,1)S(1)}, bf16[4,256,4096]{2,1,0:T(8,128)(2,1)}, u32[]{:S(2)}) copy-start(bf16[4,256,4096]{2,1,0:T(8,128)(2,1)} %get-tuple-element.19) | copy-start | bytes 25165828
  988.1 42.2 %copy-start.6 = (bf16[1024,4096]{1,0:T(8,128)(2,1)S(1)}, bf16[1024,4096]{1,0:T(8,128)(2,1)}, u32[]{:S(2)}) copy-start(bf16[1024,4096]{1,0:T(8,128)(2,1)} %attention.4) | copy-start | bytes 25165828
  1030.3 40.7 %copy-start.3 = (bf16[4,256,4096]{2,1,0:T(8,128)(2,1)S(1)}, bf16[4,256,4096]{2,1,0:T(8,128)(2,1)}, u32[]{:S(2)}) copy-start(bf16[4,256,4096]{2,1,0:T(8,128)(2,1)} %get-tuple-element.21) | copy-start | bytes 25165828
Sparse Core Ops, SparseCore 0:
  63.2 155.6 all-gather.10
  220.6 155.2 all-gather.8
  377.7 155.2 all-gather.14
  534.6 155.2 all-gather.12

commit v2 on v1

v2 whole, which is shorter than its diff:
```python
import functools

import jax
import jax.numpy as jnp
from jax import lax
from jax.experimental import pallas as pl
from jax.experimental.pallas import tpu as pltpu
from jax.sharding import PartitionSpec as P

EPS = 1e-6
THETA = 1000000.0
HD = 128
LOG2E = 1.4426950408889634
VMEM_LIMIT = 60 * 1024 * 1024
BLK = 256


def rope_tables(positions):
    half = HD // 2
    inv_freq = THETA ** (-jnp.arange(half, dtype=jnp.float32) * 2.0 / HD)
    angles = positions.astype(jnp.float32)[:, None] * inv_freq[None, :]
    cos_t, sin_t = jnp.cos(angles), jnp.sin(angles)
    return jnp.concatenate([cos_t, cos_t], axis=1), jnp.concatenate([-sin_t, sin_t], axis=1)


def head_norm_rope(raw, gain, cos_t, sin_t):
    inv = lax.rsqrt(jnp.mean(raw * raw, axis=-1, keepdims=True) + EPS)
    normed = raw * inv * gain
    return normed * cos_t + pltpu.roll(normed, HD // 2, 1) * sin_t


def kv_kernel(x_ref, g_ref, wk_ref, wv_ref, kg_ref, cos_ref, sin_ref, h_ref, kv_ref):
    wide = x_ref[...].astype(jnp.float32)
    inv = lax.rsqrt(jnp.mean(wide * wide, axis=-1, keepdims=True) + EPS)
    h_ref[...] = (wide * inv * g_ref[...]).astype(jnp.bfloat16)
    hid = h_ref[...]
    n_k = wk_ref.shape[1]
    step = 512
    for c in range(0, n_k, step):
        raw = jnp.dot(hid, wk_ref[:, c:c + step], preferred_element_type=jnp.float32)
        raw = raw.astype(jnp.bfloat16).astype(jnp.float32)
        for j in range(0, step, HD):
            k_rot = head_norm_rope(raw[:, j:j + HD], kg_ref[...], cos_ref[...], sin_ref[...])
            kv_ref[:, c + j:c + j + HD] = k_rot.astype(jnp.bfloat16)
    for c in range(0, n_k, step):
        raw = jnp.dot(hid, wv_ref[:, c:c + step], preferred_element_type=jnp.float32)
        kv_ref[:, n_k + c:n_k + c + step] = raw.astype(jnp.bfloat16)


def kv_project(x, first, n_blk, w_key, w_value, attn_gain, k_gain, cos_t, sin_t):
    d_model = x.shape[1]
    n_k = w_key.shape[1]
    rows = n_blk * BLK
    row_blk = lambda width: pl.BlockSpec((BLK, width), lambda i: (i, 0))
    full = lambda a: pl.BlockSpec(a.shape, lambda i: (0, 0), pipeline_mode=pl.Buffered(1))
    return pl.pallas_call(
        kv_kernel,
        grid=(n_blk,),
        in_specs=[pl.BlockSpec((BLK, d_model), lambda i: (first + i, 0))] + [full(a) for a in (attn_gain, w_key, w_value, k_gain, cos_t, sin_t)],
        out_specs=[row_blk(d_model), row_blk(2 * n_k)],
        out_shape=[jax.ShapeDtypeStruct((rows, d_model), jnp.bfloat16), jax.ShapeDtypeStruct((rows, 2 * n_k), jnp.bfloat16)],
        compiler_params=pltpu.CompilerParams(vmem_limit_bytes=VMEM_LIMIT, dimension_semantics=('arbitrary',)),
        cost_estimate=pl.CostEstimate(flops=4 * rows * d_model * n_k, bytes_accessed=rows * (d_model + n_k) * 4 + 4 * d_model * n_k, transcendentals=0),
        name='kv_project',
    )(x, attn_gain, w_key, w_value, k_gain, cos_t, sin_t)


def q_kernel(n_col, hid_ref, w_ref, qg_ref, cos_ref, sin_ref, q_ref, raw_s):
    i = pl.program_id(0)

    def dot(slot):
        raw_s[slot] = jnp.dot(hid_ref[...], w_ref[...], preferred_element_type=jnp.float32)

    def finish(slot):
        rows, width = q_ref.shape
        for r in range(0, rows, BLK):
            for c in range(0, width, HD):
                raw = raw_s[slot, r:r + BLK, c:c + HD].astype(jnp.bfloat16).astype(jnp.float32)
                q_ref[r:r + BLK, c:c + HD] = head_norm_rope(raw, qg_ref[...], cos_ref[...], sin_ref[...]).astype(jnp.bfloat16)

    @pl.when(i == 0)
    def _():
        dot(0)

    for slot in range(2):
        @pl.when(jnp.logical_and(jnp.logical_and(i > 0, i < n_col), i % 2 == slot))
        def _():
            dot(slot)
            finish(1 - slot)

    @pl.when(i == n_col)
    def _():
        finish((n_col - 1) % 2)


def q_project(hid, w_query, q_gain, cos_t, sin_t):
    rows, d_model = hid.shape
    bn = 512
    n_col = w_query.shape[1] // bn
    const = lambda a: pl.BlockSpec(a.shape, lambda i: (0, 0))
    return pl.pallas_call(
        functools.partial(q_kernel, n_col),
        grid=(n_col + 1,),
        in_specs=[pl.BlockSpec(hid.shape, lambda i: (0, 0), pipeline_mode=pl.Buffered(1)), pl.BlockSpec((d_model, bn), lambda i: (0, jnp.minimum(i, n_col - 1))), const(q_gain), const(cos_t), const(sin_t)],
        out_specs=pl.BlockSpec((rows, bn), lambda i: (0, jnp.maximum(i - 1, 0))),
        out_shape=jax.ShapeDtypeStruct((rows, w_query.shape[1]), jnp.bfloat16),
        scratch_shapes=[pltpu.VMEM((2, rows, bn), jnp.float32)],
        compiler_params=pltpu.CompilerParams(vmem_limit_bytes=VMEM_LIMIT, dimension_semantics=('arbitrary',)),
        cost_estimate=pl.CostEstimate(flops=2 * rows * w_query.size, bytes_accessed=2 * w_query.size + 4 * hid.size, transcendentals=0),
        name='q_project',
    )(hid, w_query, q_gain, cos_t, sin_t)


def out_kernel(o_ref, w_ref, x_ref, *rest):
    y_ref = rest[-1]
    y_ref[...] = (x_ref[...].astype(jnp.float32) + jnp.dot(o_ref[...], w_ref[...], preferred_element_type=jnp.float32)).astype(jnp.bfloat16)


def out_project(attn, w_out, x, g, so_far):
    rows, depth = attn.shape
    bn = 512
    tile = pl.BlockSpec((rows, bn), lambda i: (g, i))
    extra = [] if so_far is None else [so_far]
    return pl.pallas_call(
        out_kernel,
        grid=(w_out.shape[1] // bn,),
        in_specs=[pl.BlockSpec(attn.shape, lambda i: (0, 0), pipeline_mode=pl.Buffered(1)), pl.BlockSpec((depth, bn), lambda i: (0, i)), tile] + [pl.BlockSpec(memory_space=pl.ANY)] * len(extra),
        out_specs=tile,
        out_shape=jax.ShapeDtypeStruct(x.shape, jnp.bfloat16),
        input_output_aliases={3: 0} if extra else {},
        compiler_params=pltpu.CompilerParams(vmem_limit_bytes=VMEM_LIMIT, dimension_semantics=('arbitrary',)),
        cost_estimate=pl.CostEstimate(flops=2 * rows * w_out.size, bytes_accessed=2 * w_out.size + 6 * attn.size, transcendentals=0),
        name='out_project',
    )(attn, w_out, x, *extra)


def attn_kernel(n_group, n_head, blk, idx_ref, q_ref, k_ref, v_ref, o_ref, acc_s, m_s, l_s, s_s, p_s, a_s):
    last = idx_ref[0] // 2
    shift = (idx_ref[0] % 2) * blk
    scale = LOG2E * HD ** -0.5
    width = 2 * blk

    def load(ref, u, h):
        c = h // n_group * HD
        return ref[pl.ds(2 * u, 2), :, c:c + HD].reshape(width, HD)

    def qk(u, h):
        s_s[h % 2] = lax.dot_general(q_ref[:, h * HD:(h + 1) * HD], load(k_ref, u, h), (((1,), (1,)), ((), ())), preferred_element_type=jnp.float32)

    def fold(p):
        part = p[:, :HD]
        for j in range(HD, width, HD):
            part = part + p[:, j:j + HD]
        return part

    def soft(h, masked):
        s = s_s[h % 2]
        if masked:
            allowed = lax.broadcasted_iota(jnp.int32, s.shape, 1) <= lax.broadcasted_iota(jnp.int32, s.shape, 0) + shift
            s = jnp.where(allowed, s, -jnp.inf)
        m = jnp.broadcast_to(jnp.max(s, axis=1, keepdims=True) * scale, (blk, HD))
        if not masked:
            m_old = m_s[h]
            m = jnp.maximum(m_old, m)
            alpha = jnp.exp2(m_old - m)
            a_s[h % 2] = alpha
        p = jnp.exp2(s * scale - jnp.concatenate([m] * (width // HD), axis=1))
        m_s[h] = m
        l_s[h] = fold(p) if masked else l_s[h] * alpha + fold(p)
        p_s[h % 2] = p.astype(jnp.bfloat16)

    def pv(u, h, fresh):
        o = jnp.dot(p_s[h % 2], load(v_ref, u, h), preferred_element_type=jnp.float32)
        acc_s[h] = o if fresh else acc_s[h] * a_s[h % 2] + o

    end = n_head - 1
    qk(last, 0)
    for h in range(n_head):
        if h < end:
            qk(last, h + 1)
        else:
            qk(0, 0)
        if h > 0:
            pv(last, h - 1, True)
        soft(h, True)
    acc_s[end] = jnp.zeros_like(acc_s[end])
    a_s[end % 2] = jnp.zeros_like(a_s[end % 2])

    def body(u, _):
        for h in range(n_head):
            if h < end:
                qk(u, h + 1)
            else:
                qk(jnp.minimum(u + 1, last), 0)
            if h > 0:
                pv(u, h - 1, False)
            else:
                pv(jnp.where(u == 0, last, u - 1), end, False)
            soft(h, False)
        return 0

    lax.fori_loop(0, last, body, 0)
    pv(jnp.where(last == 0, 0, last - 1), end, False)
    for h in range(n_head):
        total = jnp.sum(l_s[h], axis=1, keepdims=True)
        o_ref[:, h * HD:(h + 1) * HD] = (acc_s[h] * (1.0 / total)).astype(jnp.bfloat16)

def attention(idx, q, kv_all, pair=2):
    n_dev, rows, kv_w = kv_all.shape
    n_kv = kv_w // (2 * HD)
    n_group = q.shape[1] // (n_kv * HD)
    n_head = pair * n_group
    blk = BLK
    qo = pl.BlockSpec((blk, n_head * HD), lambda b, h, i: (b, h))
    kv_spec = lambda off: pl.BlockSpec((n_dev, blk, pair * HD), lambda b, h, i: (0, b, off + h))
    f32 = lambda *shape: pltpu.VMEM(shape, jnp.float32)
    return pl.pallas_call(
        functools.partial(attn_kernel, n_group, n_head, blk),
        grid_spec=pltpu.PrefetchScalarGridSpec(
            num_scalar_prefetch=1,
            grid=(rows // blk, n_kv // pair),
            in_specs=[qo, kv_spec(0), kv_spec(n_kv // pair)],
            out_specs=qo,
            scratch_shapes=[f32(n_head, blk, HD)] * 3 + [f32(2, blk, 2 * blk), pltpu.VMEM((2, blk, 2 * blk), jnp.bfloat16), f32(2, blk, HD)],
        ),
        out_shape=jax.ShapeDtypeStruct(q.shape, jnp.bfloat16),
        compiler_params=pltpu.CompilerParams(vmem_limit_bytes=VMEM_LIMIT, dimension_semantics=('arbitrary', 'arbitrary')),
        cost_estimate=pl.CostEstimate(flops=8 * rows * q.shape[1] * n_dev * blk, bytes_accessed=4 * q.size + 2 * kv_all.size, transcendentals=0),
        name='attention',
    )(idx, q, kv_all, kv_all)


def solution(mesh):
    def per_device(tokens, w_query, w_key, w_value, w_out, attn_norm, q_norm, k_norm):
        n_batch, seq_loc, d_model = tokens.shape
        me = lax.axis_index('sp')
        cos_t, sin_t = rope_tables(me * seq_loc + jnp.arange(seq_loc))
        attn_gain = attn_norm.astype(jnp.float32)[None, :]
        q_gain = q_norm.astype(jnp.float32)[None, :]
        k_gain = k_norm.astype(jnp.float32)[None, :]
        idx = jnp.reshape(me, (1,)).astype(jnp.int32)
        flat = tokens.reshape(n_batch * seq_loc, d_model)
        n_kv = w_key.shape[1] // HD

        n_chunk = 4
        n_blk = n_batch // n_chunk
        hid, kv, kv_all = [], [], []
        for g in range(n_chunk):
            h_g, kv_g = kv_project(flat, g * n_blk, n_blk, w_key, w_value, attn_gain, k_gain, cos_t, sin_t)
            hid.append(h_g)
            kv.append(kv_g)
            kv_all.append(lax.all_gather(kv_g, 'sp', axis=0, tiled=False))
        out = None
        for g in range(n_chunk):
            q_g = q_project(hid[g], w_query, q_gain, cos_t, sin_t)
            out = out_project(attention(idx, q_g, kv_all[g]), w_out, flat, g, out)
        out = out.reshape(tokens.shape)
        kv_cat = jnp.concatenate(kv, axis=0)
        k_cache = kv_cat[:, :n_kv * HD].reshape(n_batch, seq_loc, n_kv, HD)
        v_cache = kv_cat[:, n_kv * HD:].reshape(n_batch, seq_loc, n_kv, HD)
        return out, k_cache, v_cache

    spec_tok = P('dp', 'sp', None)
    spec_cache = P('dp', 'sp', None, None)
    spec_mat = P(None, None)
    spec_vec = P(None)
    return jax.shard_map(per_device, mesh=mesh, in_specs=(spec_tok, spec_mat, spec_mat, spec_mat, spec_mat, spec_vec, spec_vec, spec_vec), out_specs=(spec_tok, spec_cache, spec_cache), check_vma=False)
```

time: 1400 us -> 1010 us (0.72)
  the two profiles are of different devices: /device:TPU:7 before, /device:TPU:6 now
where the time goes in v2:
time: 1010 us; the launch traced here: 1000 us
  Pallas kernels  949 us (94%)
  local copies, waits for them, and re-layouts  31.9 us (3%)
  between operations  14.3 us (1%)
    pallas_call x4, Pallas kernels, attention(): pl.pallas_call(functools.partial(attn_kernel, n_group, n_head, blk), grid...  479 us
    pallas_call x4, Pallas kernels, q_project(): pl.pallas_call(functools.partial(q_kernel, n_col), grid=(n_col + 1,), in_...  185 us
    pallas_call x4, Pallas kernels, out_project(): pl.pallas_call(out_kernel, grid=(w_out.shape[1] // bn,), in_specs=[pl.Blo...  168 us
    pallas_call x4, Pallas kernels, kv_project(): pl.pallas_call(kv_kernel, grid=(n_blk,), in_specs=[pl.BlockSpec((BLK, d_m...  116 us
    unnamed x14, local copies, waits for them, and re-layouts  31.3 us
  transfers between devices with their start and end apart: 4, of which 0 were waited for; matrix products, arithmetic and copies ran while one was open for 3% of the time, Pallas kernels for 76%

profile of v2, /device:TPU:6, one launch (start us, length us, event | category | flops | bytes accessed | tf_op | source)
XLA Modules:
  0.0 999.6 jit_solution(6496163868830468311)
XLA Ops:
  7.2 1.3 broadcast_in_dim.23
  8.6 1.2 bitcast_convert_fusion.1.kg_ref
  9.7 0.5 fusion
  10.3 0.9 pad_maximum_fusion
  11.1 29.0 %kv_project.7 = (bf16[1024,4096]{1,0:T(8,128)(2,1)}, bf16[1024,2048]{1,0:T(8,128)(2,1)}) custom-call(bf16[4096,4096]{1,0:T(8,128)(2,1)} %bitcast.22, f32[1,4096]{1,0:T(1,128)} %bitcast.33, bf16[4096,1024]{1,0:T(8,128)(2,1)} %wk_ref.7, bf16[4096,1024]{1,0:T(8,128)(2,1)} %wv_ref.7, f32[1,128]{1,0:T(1,128)} %bitcast_convert_fusion.1.kg_ref, ...), custom_call_target="tpu_custom_call" | custom-call | flops 17179869184 | bytes 37748736 | tf_op jit(solution)/shard_map/kv_project/pallas_call | solution.py:56
  40.2 29.0 %kv_project.6 = (bf16[1024,4096]{1,0:T(8,128)(2,1)}, bf16[1024,2048]{1,0:T(8,128)(2,1)}) custom-call(bf16[4096,4096]{1,0:T(8,128)(2,1)} %bitcast.23, f32[1,4096]{1,0:T(1,128)} %bitcast.34, bf16[4096,1024]{1,0:T(8,128)(2,1)} %wk_ref.7, bf16[4096,1024]{1,0:T(8,128)(2,1)} %wv_ref.7, f32[1,128]{1,0:T(1,128)} %bitcast_convert_fusion.1.kg_ref, ...), custom_call_target="tpu_custom_call" | custom-call | flops 17179869184 | bytes 37748736 | tf_op jit(solution)/shard_map/kv_project/pallas_call | solution.py:56
  69.3 0.3 all-gather.11.cloned.1.call-start
  69.6 29.0 %kv_project.5 = (bf16[1024,4096]{1,0:T(8,128)(2,1)}, bf16[1024,2048]{1,0:T(8,128)(2,1)}) custom-call(bf16[4096,4096]{1,0:T(8,128)(2,1)} %bitcast.24, f32[1,4096]{1,0:T(1,128)} %bitcast.35, bf16[4096,1024]{1,0:T(8,128)(2,1)} %wk_ref.7, bf16[4096,1024]{1,0:T(8,128)(2,1)} %wv_ref.7, f32[1,128]{1,0:T(1,128)} %bitcast_convert_fusion.1.kg_ref, ...), custom_call_target="tpu_custom_call" | custom-call | flops 17179869184 | bytes 37748736 | tf_op jit(solution)/shard_map/kv_project/pallas_call | solution.py:56
  98.7 29.0 %kv_project.4 = (bf16[1024,4096]{1,0:T(8,128)(2,1)}, bf16[1024,2048]{1,0:T(8,128)(2,1)}) custom-call(bf16[4096,4096]{1,0:T(8,128)(2,1)} %bitcast.25, f32[1,4096]{1,0:T(1,128)} %bitcast.36, bf16[4096,1024]{1,0:T(8,128)(2,1)} %wk_ref.7, bf16[4096,1024]{1,0:T(8,128)(2,1)} %wv_ref.7, f32[1,128]{1,0:T(1,128)} %bitcast_convert_fusion.1.kg_ref, ...), custom_call_target="tpu_custom_call" | custom-call | flops 17179869184 | bytes 37748736 | tf_op jit(solution)/shard_map/kv_project/pallas_call | solution.py:56
  127.7 2.7 constant_dynamic-update-slice_fusion.3
  130.4 0.8 copy-done
  131.1 0.6 constant_dynamic-update-slice_fusion.2
  131.7 0.7 copy-done.1
  132.4 0.6 constant_dynamic-update-slice_fusion.1
  133.0 0.8 copy-done.2
  133.8 0.6 constant_dynamic-update-slice_fusion
  134.4 7.3 slice_bitcast_fusion
  141.7 8.9 copy.14
  150.7 9.0 copy.15
  159.6 0.5 bitcast_convert_fusion.qg_ref
  160.1 51.7 %q_project.7.q_ref = bf16[1024,4096]{1,0:T(8,128)(2,1)} custom-call(bf16[1024,4096]{1,0:T(8,128)(2,1)} %get-tuple-element.17.hid_ref, bf16[4096,4096]{1,0:T(8,128)(2,1)} %w_ref.11, f32[1,128]{1,0:T(1,128)} %bitcast_convert_fusion.qg_ref, f32[256,128]{1,0:T(8,128)} %get-tuple-element.24.cos_ref, f32[256,128]{1,0:T(8,128)} %get-tuple-element.25.sin_ref), custom_call_target="tpu_custom_call" | custom-call | flops 34359738368 | bytes 50331648 | tf_op jit(solution)/shard_map/q_project/pallas_call | solution.py:101
  211.8 44.5 %q_project.6.q_ref = bf16[1024,4096]{1,0:T(8,128)(2,1)} custom-call(bf16[1024,4096]{1,0:T(8,128)(2,1)} %get-tuple-element.15.hid_ref, bf16[4096,4096]{1,0:T(8,128)(2,1)} %w_ref.11, f32[1,128]{1,0:T(1,128)} %bitcast_convert_fusion.qg_ref, f32[256,128]{1,0:T(8,128)} %get-tuple-element.24.cos_ref, f32[256,128]{1,0:T(8,128)} %get-tuple-element.25.sin_ref), custom_call_target="tpu_custom_call" | custom-call | flops 34359738368 | bytes 50331648 | tf_op jit(solution)/shard_map/q_project/pallas_call | solution.py:101
  256.4 44.7 %q_project.5.q_ref = bf16[1024,4096]{1,0:T(8,128)(2,1)} custom-call(bf16[1024,4096]{1,0:T(8,128)(2,1)} %get-tuple-element.13.hid_ref, bf16[4096,4096]{1,0:T(8,128)(2,1)} %w_ref.11, f32[1,128]{1,0:T(1,128)} %bitcast_convert_fusion.qg_ref, f32[256,128]{1,0:T(8,128)} %get-tuple-element.24.cos_ref, f32[256,128]{1,0:T(8,128)} %get-tuple-element.25.sin_ref), custom_call_target="tpu_custom_call" | custom-call | flops 34359738368 | bytes 50331648 | tf_op jit(solution)/shard_map/q_project/pallas_call | solution.py:101
  301.0 44.5 %q_project.4.q_ref = bf16[1024,4096]{1,0:T(8,128)(2,1)} custom-call(bf16[1024,4096]{1,0:T(8,128)(2,1)} %get-tuple-element.11.hid_ref, bf16[4096,4096]{1,0:T(8,128)(2,1)} %w_ref.11, f32[1,128]{1,0:T(1,128)} %bitcast_convert_fusion.qg_ref, f32[256,128]{1,0:T(8,128)} %get-tuple-element.24.cos_ref, f32[256,128]{1,0:T(8,128)} %get-tuple-element.25.sin_ref), custom_call_target="tpu_custom_call" | custom-call | flops 34359738368 | bytes 50331648 | tf_op jit(solution)/shard_map/q_project/pallas_call | solution.py:101
  345.5 119.9 %attention.7.o_ref = bf16[1024,4096]{1,0:T(8,128)(2,1)} custom-call(s32[1]{0:T(128)} %bitcast.idx_ref, bf16[1024,4096]{1,0:T(8,128)(2,1)} %q_project.7.q_ref, bf16[8,1024,2048]{2,1,0:T(8,128)(2,1)} %bitcast.37, bf16[8,1024,2048]{2,1,0:T(8,128)(2,1)} %bitcast.38), custom_call_target="tpu_custom_call" | custom-call | flops 68719476736 | bytes 50331648 | tf_op jit(solution)/shard_map/attention/pallas_call | solution.py:217
  465.4 42.0 %out_project.4.rest_0_ = bf16[4096,4096]{1,0:T(8,128)(2,1)} custom-call(bf16[1024,4096]{1,0:T(8,128)(2,1)} %attention.7.o_ref, bf16[4096,4096]{1,0:T(8,128)(2,1)} %w_ref.15, bf16[4096,4096]{1,0:T(8,128)(2,1)} %bitcast.26), custom_call_target="tpu_custom_call" | custom-call | flops 34359738368 | bytes 58720256 | tf_op jit(solution)/shard_map/out_project/pallas_call | solution.py:124
  507.4 119.7 %attention.6.o_ref = bf16[1024,4096]{1,0:T(8,128)(2,1)} custom-call(s32[1]{0:T(128)} %bitcast.idx_ref, bf16[1024,4096]{1,0:T(8,128)(2,1)} %q_project.6.q_ref, bf16[8,1024,2048]{2,1,0:T(8,128)(2,1)} %bitcast.39, bf16[8,1024,2048]{2,1,0:T(8,128)(2,1)} %bitcast.40), custom_call_target="tpu_custom_call" | custom-call | flops 68719476736 | bytes 50331648 | tf_op jit(solution)/shard_map/attention/pallas_call | solution.py:217
  627.1 42.0 %out_project.5.rest_0_ = bf16[4096,4096]{1,0:T(8,128)(2,1)} custom-call(bf16[1024,4096]{1,0:T(8,128)(2,1)} %attention.6.o_ref, bf16[4096,4096]{1,0:T(8,128)(2,1)} %w_ref.15, bf16[4096,4096]{1,0:T(8,128)(2,1)} %bitcast.27, bf16[4096,4096]{1,0:T(8,128)(2,1)} %out_project.4.rest_0_), custom_call_target="tpu_custom_call", output_to_operand_aliasing={{}: (3, {})} | custom-call | flops 34359738368 | bytes 58720256 | tf_op jit(solution)/shard_map/out_project/pallas_call | solution.py:124
  669.0 120.0 %attention.5.o_ref = bf16[1024,4096]{1,0:T(8,128)(2,1)} custom-call(s32[1]{0:T(128)} %bitcast.idx_ref, bf16[1024,4096]{1,0:T(8,128)(2,1)} %q_project.5.q_ref, bf16[8,1024,2048]{2,1,0:T(8,128)(2,1)} %bitcast.41, bf16[8,1024,2048]{2,1,0:T(8,128)(2,1)} %bitcast.42), custom_call_target="tpu_custom_call" | custom-call | flops 68719476736 | bytes 50331648 | tf_op jit(solution)/shard_map/attention/pallas_call | solution.py:217
  789.0 42.0 %out_project.6.rest_0_ = bf16[4096,4096]{1,0:T(8,128)(2,1)} custom-call(bf16[1024,4096]{1,0:T(8,128)(2,1)} %attention.5.o_ref, bf16[4096,4096]{1,0:T(8,128)(2,1)} %w_ref.15, bf16[4096,4096]{1,0:T(8,128)(2,1)} %bitcast.28, bf16[4096,4096]{1,0:T(8,128)(2,1)} %out_project.5.rest_0_), custom_call_target="tpu_custom_call", output_to_operand_aliasing={{}: (3, {})} | custom-call | flops 34359738368 | bytes 58720256 | tf_op jit(solution)/shard_map/out_project/pallas_call | solution.py:124
  831.0 119.7 %attention.4.o_ref = bf16[1024,4096]{1,0:T(8,128)(2,1)} custom-call(s32[1]{0:T(128)} %bitcast.idx_ref, bf16[1024,4096]{1,0:T(8,128)(2,1)} %q_project.4.q_ref, bf16[8,1024,2048]{2,1,0:T(8,128)(2,1)} %bitcast.43, bf16[8,1024,2048]{2,1,0:T(8,128)(2,1)} %bitcast.44), custom_call_target="tpu_custom_call" | custom-call | flops 68719476736 | bytes 50331648 | tf_op jit(solution)/shard_map/attention/pallas_call | solution.py:217
  950.6 42.0 %out_project.7 = bf16[4096,4096]{1,0:T(8,128)(2,1)} custom-call(bf16[1024,4096]{1,0:T(8,128)(2,1)} %attention.4.o_ref, bf16[4096,4096]{1,0:T(8,128)(2,1)} %w_ref.15, bf16[4096,4096]{1,0:T(8,128)(2,1)} %bitcast.29, bf16[4096,4096]{1,0:T(8,128)(2,1)} %out_project.6.rest_0_), custom_call_target="tpu_custom_call", output_to_operand_aliasing={{}: (3, {})} | custom-call | flops 34359738368 | bytes 58720256 | tf_op jit(solution)/shard_map/out_project/pallas_call | solution.py:124
  (18 shorter events, 0.2 us)
Async XLA Ops:
  7.2 338.3 %all-gather.15.cloned.1.call-start = ((), (), s32[]{:S(2)}) async-start(), calls=%async_computation.3 | async-start | bytes 37748736 | tf_op jit(solution)/shard_map/all_gather | solution.py:252
  40.2 467.2 %all-gather.13.cloned.1.call-start = ((), (), s32[]{:S(2)}) async-start(), calls=%async_computation.2 | async-start | bytes 37748736 | tf_op jit(solution)/shard_map/all_gather | solution.py:252
  69.3 599.8 %all-gather.11.cloned.1.call-start = ((), (), s32[]{:S(2)}) async-start(), calls=%async_computation.1 | async-start | bytes 37748736 | tf_op jit(solution)/shard_map/all_gather | solution.py:252
  98.6 732.4 %all-gather.9.cloned.1.call-start = ((), (), s32[]{:S(2)}) async-start(), calls=%async_computation | async-start | bytes 37748736 | tf_op jit(solution)/shard_map/all_gather | solution.py:252
  127.7 3.5 copy-start
  127.7 4.7 copy-start.1
  131.1 2.7 copy-start.2
  150.7 9.0 copy-start.3
Sparse Core Ops, SparseCore 0:
  40.3 155.3 all-gather.14
  197.5 155.1 all-gather.12
  354.5 155.2 all-gather.10
  511.4 155.2 all-gather.8

commit v3 on v2

v3 whole, which is shorter than its diff:
```python
import functools

import jax
import jax.numpy as jnp
from jax import lax
from jax.experimental import pallas as pl
from jax.experimental.pallas import tpu as pltpu
from jax.sharding import PartitionSpec as P

EPS = 1e-6
THETA = 1000000.0
HD = 128
LOG2E = 1.4426950408889634
VMEM_LIMIT = 60 * 1024 * 1024
BLK = 256
PLAN = ('heads', 'heads', 'keys', 'keys')


def rope_tables(positions):
    half = HD // 2
    inv_freq = THETA ** (-jnp.arange(half, dtype=jnp.float32) * 2.0 / HD)
    angles = positions.astype(jnp.float32)[:, None] * inv_freq[None, :]
    cos_t, sin_t = jnp.cos(angles), jnp.sin(angles)
    return jnp.concatenate([cos_t, cos_t], axis=1), jnp.concatenate([-sin_t, sin_t], axis=1)


def head_norm_rope(raw, gain, cos_t, sin_t):
    inv = lax.rsqrt(jnp.mean(raw * raw, axis=-1, keepdims=True) + EPS)
    normed = raw * inv * gain
    return normed * cos_t + pltpu.roll(normed, HD // 2, 1) * sin_t


def kv_kernel(x_ref, g_ref, wk_ref, wv_ref, kg_ref, cos_ref, sin_ref, h_ref, kv_ref):
    rows, n_k = x_ref.shape[0], wk_ref.shape[1]
    for r in range(0, rows, 128):
        wide = x_ref[r:r + 128].astype(jnp.float32)
        inv = lax.rsqrt(jnp.mean(wide * wide, axis=-1, keepdims=True) + EPS)
        h_ref[r:r + 128] = (wide * inv * g_ref[...]).astype(jnp.bfloat16)
    step = 512
    for c in range(0, n_k, step):
        raw = jnp.dot(h_ref[...], wk_ref[:, c:c + step], preferred_element_type=jnp.float32).astype(jnp.bfloat16)
        for j in range(0, step, HD):
            for r in range(0, rows, BLK):
                k_rot = head_norm_rope(raw[r:r + BLK, j:j + HD].astype(jnp.float32), kg_ref[...], cos_ref[...], sin_ref[...])
                kv_ref[(c + j) // HD, r:r + BLK, :HD] = k_rot.astype(jnp.bfloat16)
    for c in range(0, n_k, step):
        raw = jnp.dot(h_ref[...], wv_ref[:, c:c + step], preferred_element_type=jnp.float32).astype(jnp.bfloat16)
        for j in range(0, step, HD):
            kv_ref[(c + j) // HD, :, HD:] = raw[:, j:j + HD]


def kv_project(x, first, n_prompt, w_key, w_value, attn_gain, k_gain, cos_t, sin_t):
    d_model = x.shape[1]
    n_k = w_key.shape[1]
    rows = n_prompt * BLK
    bm = 2 * BLK if n_prompt % 2 == 0 and first % 2 == 0 else BLK
    off = first * BLK // bm
    full = lambda a: pl.BlockSpec(a.shape, lambda i: (0, 0), pipeline_mode=pl.Buffered(1))
    return pl.pallas_call(
        kv_kernel,
        grid=(rows // bm,),
        in_specs=[pl.BlockSpec((bm, d_model), lambda i: (off + i, 0))] + [full(a) for a in (attn_gain, w_key, w_value, k_gain, cos_t, sin_t)],
        out_specs=[pl.BlockSpec((bm, d_model), lambda i: (i, 0)), pl.BlockSpec((n_k // HD, bm, 2 * HD), lambda i: (0, i, 0))],
        out_shape=[jax.ShapeDtypeStruct((rows, d_model), jnp.bfloat16), jax.ShapeDtypeStruct((n_k // HD, rows, 2 * HD), jnp.bfloat16)],
        compiler_params=pltpu.CompilerParams(vmem_limit_bytes=VMEM_LIMIT, dimension_semantics=('arbitrary',)),
        cost_estimate=pl.CostEstimate(flops=4 * rows * d_model * n_k, bytes_accessed=rows * (d_model + n_k) * 4 + 4 * d_model * n_k, transcendentals=0),
        name='kv_project',
    )(x, attn_gain, w_key, w_value, k_gain, cos_t, sin_t)


def q_kernel(n_col, hid_ref, w_ref, qg_ref, cos_ref, sin_ref, q_ref, raw_s):
    i = pl.program_id(0)

    def dot(slot):
        raw_s[slot] = jnp.dot(hid_ref[...], w_ref[...], preferred_element_type=jnp.float32)

    def finish(slot):
        rows, width = q_ref.shape
        for r in range(0, rows, BLK):
            for c in range(0, width, HD):
                raw = raw_s[slot, r:r + BLK, c:c + HD].astype(jnp.bfloat16).astype(jnp.float32)
                q_ref[r:r + BLK, c:c + HD] = head_norm_rope(raw, qg_ref[...], cos_ref[...], sin_ref[...]).astype(jnp.bfloat16)

    @pl.when(i == 0)
    def _():
        dot(0)

    for slot in range(2):
        @pl.when(jnp.logical_and(jnp.logical_and(i > 0, i < n_col), i % 2 == slot))
        def _():
            dot(slot)
            finish(1 - slot)

    @pl.when(i == n_col)
    def _():
        finish((n_col - 1) % 2)


def q_project(hid, n_kv, w_query, q_gain, cos_t, sin_t):
    rows, d_model = hid.shape
    bn = w_query.shape[1] // n_kv
    n_col = w_query.shape[1] // bn
    const = lambda a: pl.BlockSpec(a.shape, lambda i: (0, 0))
    return pl.pallas_call(
        functools.partial(q_kernel, n_col),
        grid=(n_col + 1,),
        in_specs=[pl.BlockSpec(hid.shape, lambda i: (0, 0), pipeline_mode=pl.Buffered(1)), pl.BlockSpec((d_model, bn), lambda i: (0, jnp.minimum(i, n_col - 1))), const(q_gain), const(cos_t), const(sin_t)],
        out_specs=pl.BlockSpec((None, rows, bn), lambda i: (jnp.maximum(i - 1, 0), 0, 0)),
        out_shape=jax.ShapeDtypeStruct((n_col, rows, bn), jnp.bfloat16),
        scratch_shapes=[pltpu.VMEM((2, rows, bn), jnp.float32)],
        compiler_params=pltpu.CompilerParams(vmem_limit_bytes=VMEM_LIMIT, dimension_semantics=('arbitrary',)),
        cost_estimate=pl.CostEstimate(flops=2 * rows * w_query.size, bytes_accessed=2 * w_query.size + 4 * hid.size, transcendentals=0),
        name='q_project',
    )(hid, w_query, q_gain, cos_t, sin_t)


def out_kernel(o_ref, w_ref, x_ref, *rest):
    y_ref, flat_s, sem = rest[-3:]
    width = o_ref.shape[2]

    @pl.when(pl.program_id(0) == 0)
    def _():
        copies = [pltpu.make_async_copy(o_ref.at[h], flat_s.at[:, h * width:(h + 1) * width], sem.at[h]) for h in range(o_ref.shape[0])]
        for copy in copies:
            copy.start()
        for copy in copies:
            copy.wait()

    y_ref[...] = (x_ref[...].astype(jnp.float32) + jnp.dot(flat_s[...], w_ref[...], preferred_element_type=jnp.float32)).astype(jnp.bfloat16)


def out_project(attn, w_out, x, first, so_far):
    n_kv, rows, width = attn.shape
    depth = n_kv * width
    bn = 512
    g = first * BLK // rows
    tile = pl.BlockSpec((rows, bn), lambda i: (g, i))
    extra = [] if so_far is None else [so_far]
    anywhere = pl.BlockSpec(memory_space=pl.ANY)
    return pl.pallas_call(
        out_kernel,
        grid=(w_out.shape[1] // bn,),
        in_specs=[anywhere, pl.BlockSpec((depth, bn), lambda i: (0, i)), tile] + [anywhere] * len(extra),
        out_specs=tile,
        out_shape=jax.ShapeDtypeStruct(x.shape, jnp.bfloat16),
        input_output_aliases={3: 0} if extra else {},
        scratch_shapes=[pltpu.VMEM((rows, depth), jnp.bfloat16), pltpu.SemaphoreType.DMA((n_kv,))],
        compiler_params=pltpu.CompilerParams(vmem_limit_bytes=VMEM_LIMIT, dimension_semantics=('arbitrary',)),
        cost_estimate=pl.CostEstimate(flops=2 * rows * w_out.size, bytes_accessed=2 * w_out.size + 6 * attn.size, transcendentals=0),
        name='out_project',
    )(attn, w_out, x, *extra)


def attn_kernel(by_head, n_group, idx_ref, q_ref, k_ref, v_ref, o_ref, acc_s, m_s, l_s, s_s, p_s, a_s):
    piece = pl.program_id(1) if by_head else idx_ref[0]
    blk = q_ref.shape[1]
    n_head = q_ref.shape[0] * n_group
    last = piece // 2
    shift = (piece % 2) * blk
    scale = LOG2E * HD ** -0.5
    width = 2 * blk

    def load(ref, u, h):
        return ref[pl.ds(2 * u, 2), h // n_group].reshape(width, HD)

    def cols(h):
        return h // n_group, slice(None), slice(h % n_group * HD, (h % n_group + 1) * HD)

    def qk(u, h):
        s_s[h % 2] = lax.dot_general(q_ref[cols(h)], load(k_ref, u, h), (((1,), (1,)), ((), ())), preferred_element_type=jnp.float32)

    def fold(p):
        part = p[:, :HD]
        for j in range(HD, width, HD):
            part = part + p[:, j:j + HD]
        return part

    def soft(h, masked):
        s = s_s[h % 2]
        if masked:
            allowed = lax.broadcasted_iota(jnp.int32, s.shape, 1) <= lax.broadcasted_iota(jnp.int32, s.shape, 0) + shift
            s = jnp.where(allowed, s, -jnp.inf)
        m = jnp.broadcast_to(jnp.max(s, axis=1, keepdims=True) * scale, (blk, HD))
        if not masked:
            m_old = m_s[h]
            m = jnp.maximum(m_old, m)
            alpha = jnp.exp2(m_old - m)
            a_s[h % 2] = alpha
        p = jnp.exp2(s * scale - jnp.concatenate([m] * (width // HD), axis=1))
        m_s[h] = m
        l_s[h] = fold(p) if masked else l_s[h] * alpha + fold(p)
        p_s[h % 2] = p.astype(jnp.bfloat16)

    def pv(u, h, fresh):
        o = jnp.dot(p_s[h % 2], load(v_ref, u, h), preferred_element_type=jnp.float32)
        acc_s[h] = o if fresh else acc_s[h] * a_s[h % 2] + o

    end = n_head - 1
    qk(last, 0)
    for h in range(n_head):
        if h < end:
            qk(last, h + 1)
        else:
            qk(0, 0)
        if h > 0:
            pv(last, h - 1, True)
        soft(h, True)
    acc_s[end] = jnp.zeros_like(acc_s[end])
    a_s[end % 2] = jnp.zeros_like(a_s[end % 2])

    def body(u, _):
        for h in range(n_head):
            if h < end:
                qk(u, h + 1)
            else:
                qk(jnp.minimum(u + 1, last), 0)
            if h > 0:
                pv(u, h - 1, False)
            else:
                pv(jnp.where(u == 0, last, u - 1), end, False)
            soft(h, False)
        return 0

    lax.fori_loop(0, last, body, 0)
    pv(jnp.where(last == 0, 0, last - 1), end, False)
    for h in range(n_head):
        total = jnp.sum(l_s[h], axis=1, keepdims=True)
        o_ref[cols(h)] = (acc_s[h] * (1.0 / total)).astype(jnp.bfloat16)

def attention(idx, q, kv, by_head):
    n_piece, n_kv, rows, _ = kv.shape
    n_slab, _, width = q.shape
    n_group = width // HD
    pair = 1 if by_head else 2
    n_head = pair * n_group
    qo = pl.BlockSpec((pair, BLK, width), lambda b, h, i: (h, b, 0))
    kv_spec = lambda half: pl.BlockSpec((n_piece, pair, BLK, HD), lambda b, h, i: (0, 0 if by_head else h, b, half))
    f32 = lambda *shape: pltpu.VMEM(shape, jnp.float32)
    work = 5 if by_head else n_piece
    return pl.pallas_call(
        functools.partial(attn_kernel, by_head, n_group),
        grid_spec=pltpu.PrefetchScalarGridSpec(
            num_scalar_prefetch=1,
            grid=(rows // BLK, n_slab // pair),
            in_specs=[qo, kv_spec(0), kv_spec(1)],
            out_specs=qo,
            scratch_shapes=[f32(n_head, BLK, HD)] * 3 + [f32(2, BLK, 2 * BLK), pltpu.VMEM((2, BLK, 2 * BLK), jnp.bfloat16), f32(2, BLK, HD)],
        ),
        out_shape=jax.ShapeDtypeStruct(q.shape, jnp.bfloat16),
        compiler_params=pltpu.CompilerParams(vmem_limit_bytes=VMEM_LIMIT, dimension_semantics=('arbitrary', 'arbitrary')),
        cost_estimate=pl.CostEstimate(flops=8 * q.size * work * BLK, bytes_accessed=4 * q.size + 2 * kv.size, transcendentals=0),
        name='attention',
    )(idx, q, kv, kv)


def solution(mesh):
    def per_device(tokens, w_query, w_key, w_value, w_out, attn_norm, q_norm, k_norm):
        n_batch, seq_loc, d_model = tokens.shape
        me = lax.axis_index('sp')
        cos_t, sin_t = rope_tables(me * seq_loc + jnp.arange(seq_loc))
        attn_gain = attn_norm.astype(jnp.float32)[None, :]
        q_gain = q_norm.astype(jnp.float32)[None, :]
        k_gain = k_norm.astype(jnp.float32)[None, :]
        idx = jnp.reshape(me, (1,)).astype(jnp.int32)
        flat = tokens.reshape(n_batch * seq_loc, d_model)
        n_kv = w_key.shape[1] // HD

        n_chunk = len(PLAN)
        n_prompt = n_batch // n_chunk
        order = sorted(range(n_chunk), key=lambda g: PLAN[g] != 'heads')
        swap = lambda a: lax.all_to_all(a, 'sp', 0, 0, tiled=True)
        q, kv, moved, mixed = {}, {}, {}, {}
        hid = {}
        for g in order:
            hid[g], kv[g] = kv_project(flat, g * n_prompt, n_prompt, w_key, w_value, attn_gain, k_gain, cos_t, sin_t)
            if PLAN[g] == 'heads':
                moved[g] = swap(kv[g])[:, None]
                q[g] = swap(q_project(hid[g], n_kv, w_query, q_gain, cos_t, sin_t))
            else:
                moved[g] = lax.all_gather(kv[g], 'sp', axis=0, tiled=False)
        for g in order:
            if PLAN[g] == 'heads':
                mixed[g] = swap(attention(idx, q[g], moved[g], True))
            else:
                mixed[g] = attention(idx, q_project(hid[g], n_kv, w_query, q_gain, cos_t, sin_t), moved[g], False)
        out = None
        for g in reversed(order):
            out = out_project(mixed[g], w_out, flat, g * n_prompt, out)
        out = out.reshape(tokens.shape)

        def cache(half):
            parts = [jnp.swapaxes(kv[g][:, :, half * HD:(half + 1) * HD], 0, 1) for g in range(n_chunk)]
            return jnp.concatenate(parts, axis=0).reshape(n_batch, seq_loc, n_kv, HD)

        k_cache, v_cache = cache(0), cache(1)
        return out, k_cache, v_cache

    spec_tok = P('dp', 'sp', None)
    spec_cache = P('dp', 'sp', None, None)
    spec_mat = P(None, None)
    spec_vec = P(None)
    return jax.shard_map(per_device, mesh=mesh, in_specs=(spec_tok, spec_mat, spec_mat, spec_mat, spec_mat, spec_vec, spec_vec, spec_vec), out_specs=(spec_tok, spec_cache, spec_cache), check_vma=False)
```

time: 1010 us -> 1110 us (1.099)
  the two profiles are of different devices: /device:TPU:6 before, /device:TPU:0 now
where the time goes in v3:
time: 1110 us; the launch traced here: 1100 us
  Pallas kernels  692 us (62%)
  starting transfers between devices  174 us (16%)
  waiting for transfers between devices  159 us (14%)
  local copies, waits for them, and re-layouts  44.6 us (4%)
  other arithmetic  14.9 us (1%)
  between operations  14.7 us (1%)
    pallas_call x4, Pallas kernels, attention(): pl.pallas_call(functools.partial(attn_kernel, by_head, n_group), grid_spe...  224 us
    pallas_call x4, Pallas kernels, q_project(): pl.pallas_call(functools.partial(q_kernel, n_col), grid=(n_col + 1,), in_...  177 us
    pallas_call x4, Pallas kernels, out_project(): pl.pallas_call(out_kernel, grid=(w_out.shape[1] // bn,), in_specs=[anywhe...  175 us
    all_to_all x6, starting transfers between devices, per_device(): swap = lambda a: lax.all_to_all(a, 'sp', 0, 0, tiled=True)  174 us
    all_to_all x6, waiting for transfers between devices, per_device(): swap = lambda a: lax.all_to_all(a, 'sp', 0, 0, tiled=True)  159 us
    pallas_call x4, Pallas kernels, kv_project(): pl.pallas_call(kv_kernel, grid=(rows // bm,), in_specs=[pl.BlockSpec((bm,...  115 us
    unnamed x12, local copies, waits for them, and re-layouts  28.7 us
  transfers between devices with their start and end apart: 8, of which 4 were waited for; matrix products, arithmetic and copies ran while one was open for 5% of the time, Pallas kernels for 56%

profile of v3, /device:TPU:0, one launch (start us, length us, event | category | flops | bytes accessed | tf_op | source)
XLA Modules:
  0.0 1098.9 jit_solution(16950887207952548646)
XLA Ops:
  11.1 28.7 %kv_project.7 = (bf16[1024,4096]{1,0:T(8,128)(2,1)}, bf16[8,1024,256]{2,1,0:T(8,128)(2,1)}) custom-call(bf16[4096,4096]{1,0:T(8,128)(2,1)} %bitcast.32, f32[1,4096]{1,0:T(1,128)} %bitcast.43, bf16[4096,1024]{1,0:T(8,128)(2,1)} %wk_ref.7, bf16[4096,1024]{1,0:T(8,128)(2,1)} %wv_ref.7, f32[1,128]{1,0:T(1,128)} %bitcast_convert_fusion.1.kg_ref, ...), custom_call_target="tpu_custom_call" | custom-call | flops 17179869184 | bytes 37748736 | tf_op jit(solution)/shard_map/kv_project/pallas_call | solution.py:59
  40.1 28.7 %kv_project.6 = (bf16[1024,4096]{1,0:T(8,128)(2,1)}, bf16[8,1024,256]{2,1,0:T(8,128)(2,1)}) custom-call(bf16[4096,4096]{1,0:T(8,128)(2,1)} %bitcast.33, f32[1,4096]{1,0:T(1,128)} %bitcast.44, bf16[4096,1024]{1,0:T(8,128)(2,1)} %wk_ref.7, bf16[4096,1024]{1,0:T(8,128)(2,1)} %wv_ref.7, f32[1,128]{1,0:T(1,128)} %bitcast_convert_fusion.1.kg_ref, ...), custom_call_target="tpu_custom_call" | custom-call | flops 17179869184 | bytes 37748736 | tf_op jit(solution)/shard_map/kv_project/pallas_call | solution.py:59
  68.9 29.0 %kv_project.5 = (bf16[1024,4096]{1,0:T(8,128)(2,1)}, bf16[8,1024,256]{2,1,0:T(8,128)(2,1)}) custom-call(bf16[4096,4096]{1,0:T(8,128)(2,1)} %bitcast.34, f32[1,4096]{1,0:T(1,128)} %bitcast.45, bf16[4096,1024]{1,0:T(8,128)(2,1)} %wk_ref.7, bf16[4096,1024]{1,0:T(8,128)(2,1)} %wv_ref.7, f32[1,128]{1,0:T(1,128)} %bitcast_convert_fusion.1.kg_ref, ...), custom_call_target="tpu_custom_call" | custom-call | flops 17179869184 | bytes 37748736 | tf_op jit(solution)/shard_map/kv_project/pallas_call | solution.py:59
  97.8 4.6 all-to-all-start.4
  102.4 4.0 slice_bitcast_fusion.2
  109.5 28.7 %kv_project.4 = (bf16[1024,4096]{1,0:T(8,128)(2,1)}, bf16[8,1024,256]{2,1,0:T(8,128)(2,1)}) custom-call(bf16[4096,4096]{1,0:T(8,128)(2,1)} %bitcast.35, f32[1,4096]{1,0:T(1,128)} %bitcast.46, bf16[4096,1024]{1,0:T(8,128)(2,1)} %wk_ref.7, bf16[4096,1024]{1,0:T(8,128)(2,1)} %wv_ref.7, f32[1,128]{1,0:T(1,128)} %bitcast_convert_fusion.1.kg_ref, ...), custom_call_target="tpu_custom_call" | custom-call | flops 17179869184 | bytes 37748736 | tf_op jit(solution)/shard_map/kv_project/pallas_call | solution.py:59
  138.2 58.4 %all-to-all-done.4 = bf16[8,1024,256]{2,1,0:T(8,128)(2,1)} async-done(((bf16[8,1024,256]{2,1,0:T(8,128)(2,1)}), bf16[8,1024,256]{2,1,0:T(8,128)(2,1)}, u32[]{:S(2)}, u32[]{:S(2)}) %all-to-all-start.4) | async-done | bytes 4194336 | tf_op jit(solution)/shard_map/all_to_all | solution.py:271
  196.7 3.7 all-to-all-start.1
  201.0 4.7 slice_bitcast_fusion
  205.7 44.3 %q_project.5 = bf16[8,1024,512]{2,1,0:T(8,128)(2,1)} custom-call(bf16[1024,4096]{1,0:T(8,128)(2,1)} %get-tuple-element.13.hid_ref, bf16[4096,4096]{1,0:T(8,128)(2,1)} %w_ref.11, f32[1,128]{1,0:T(1,128)} %bitcast_convert_fusion.qg_ref, f32[256,128]{1,0:T(8,128)} %get-tuple-element.36.cos_ref, f32[256,128]{1,0:T(8,128)} %get-tuple-element.37.sin_ref), custom_call_target="tpu_custom_call" | custom-call | flops 34359738368 | bytes 50331648 | tf_op jit(solution)/shard_map/q_project/pallas_call | solution.py:104
  250.0 35.5 %all-to-all-done.1 = bf16[8,1024,256]{2,1,0:T(8,128)(2,1)} async-done(((bf16[8,1024,256]{2,1,0:T(8,128)(2,1)}), bf16[8,1024,256]{2,1,0:T(8,128)(2,1)}, u32[]{:S(2)}, u32[]{:S(2)}) %all-to-all-start.1) | async-done | bytes 4194336 | tf_op jit(solution)/shard_map/all_to_all | solution.py:271
  285.5 3.9 all-to-all-start.3
  289.4 4.0 slice_bitcast_fusion.3
  297.8 44.2 %q_project.7.q_ref = bf16[8,1024,512]{2,1,0:T(8,128)(2,1)} custom-call(bf16[1024,4096]{1,0:T(8,128)(2,1)} %get-tuple-element.17.hid_ref, bf16[4096,4096]{1,0:T(8,128)(2,1)} %w_ref.11, f32[1,128]{1,0:T(1,128)} %bitcast_convert_fusion.qg_ref, f32[256,128]{1,0:T(8,128)} %get-tuple-element.36.cos_ref, f32[256,128]{1,0:T(8,128)} %get-tuple-element.37.sin_ref), custom_call_target="tpu_custom_call" | custom-call | flops 34359738368 | bytes 50331648 | tf_op jit(solution)/shard_map/q_project/pallas_call | solution.py:104
  342.1 44.4 %q_project.4 = bf16[8,1024,512]{2,1,0:T(8,128)(2,1)} custom-call(bf16[1024,4096]{1,0:T(8,128)(2,1)} %get-tuple-element.11.hid_ref, bf16[4096,4096]{1,0:T(8,128)(2,1)} %w_ref.11, f32[1,128]{1,0:T(1,128)} %bitcast_convert_fusion.qg_ref, f32[256,128]{1,0:T(8,128)} %get-tuple-element.36.cos_ref, f32[256,128]{1,0:T(8,128)} %get-tuple-element.37.sin_ref), custom_call_target="tpu_custom_call" | custom-call | flops 34359738368 | bytes 50331648 | tf_op jit(solution)/shard_map/q_project/pallas_call | solution.py:104
  386.5 41.7 %all-to-all-done.3.q_ref = bf16[8,1024,512]{2,1,0:T(8,128)(2,1)} async-done(((bf16[8,1024,512]{2,1,0:T(8,128)(2,1)}), bf16[8,1024,512]{2,1,0:T(8,128)(2,1)}, u32[]{:S(2)}, u32[]{:S(2)}) %all-to-all-start.3) | async-done | bytes 8388640 | tf_op jit(solution)/shard_map/all_to_all | solution.py:271
  428.2 3.7 all-to-all-start
  431.9 6.8 pad_maximum_fusion.1
  438.7 13.9 %copy.16 = bf16[16,256,8,128]{3,2,1,0:T(8,128)(2,1)} copy(bf16[16,256,8,128]{3,1,0,2:T(8,128)(2,1)} %bitcast.41) | data formatting | bytes 16777216
  452.6 14.0 %copy.17 = bf16[16,256,8,128]{3,2,1,0:T(8,128)(2,1)} copy(bf16[16,256,8,128]{3,1,0,2:T(8,128)(2,1)} %bitcast.42) | data formatting | bytes 16777216
  466.6 44.3 %q_project.6.q_ref = bf16[8,1024,512]{2,1,0:T(8,128)(2,1)} custom-call(bf16[1024,4096]{1,0:T(8,128)(2,1)} %get-tuple-element.15.hid_ref, bf16[4096,4096]{1,0:T(8,128)(2,1)} %w_ref.11, f32[1,128]{1,0:T(1,128)} %bitcast_convert_fusion.qg_ref, f32[256,128]{1,0:T(8,128)} %get-tuple-element.36.cos_ref, f32[256,128]{1,0:T(8,128)} %get-tuple-element.37.sin_ref), custom_call_target="tpu_custom_call" | custom-call | flops 34359738368 | bytes 50331648 | tf_op jit(solution)/shard_map/q_project/pallas_call | solution.py:104
  510.8 77.9 %attention.5 = bf16[8,1024,512]{2,1,0:T(8,128)(2,1)} custom-call(s32[1]{0:T(128)} %bitcast.idx_ref, bf16[8,1024,512]{2,1,0:T(8,128)(2,1)} %all-to-all-done.3.q_ref, bf16[8,1,1024,256]{3,2,1,0:T(8,128)(2,1)} %bitcast.8.k_ref.v_ref, bf16[8,1,1024,256]{3,2,1,0:T(8,128)(2,1)} %bitcast.8.k_ref.v_ref), custom_call_target="tpu_custom_call" | custom-call | flops 42949672960 | bytes 20971520 | tf_op jit(solution)/shard_map/attention/pallas_call | solution.py:240
  588.8 23.4 %all-to-all-done.q_ref = bf16[8,1024,512]{2,1,0:T(8,128)(2,1)} async-done(((bf16[8,1024,512]{2,1,0:T(8,128)(2,1)}), bf16[8,1024,512]{2,1,0:T(8,128)(2,1)}, u32[]{:S(2)}, u32[]{:S(2)}) %all-to-all-start) | async-done | bytes 8388640 | tf_op jit(solution)/shard_map/all_to_all | solution.py:271
  612.2 3.7 all-to-all-start.5
  615.9 77.8 %attention.4 = bf16[8,1024,512]{2,1,0:T(8,128)(2,1)} custom-call(s32[1]{0:T(128)} %bitcast.idx_ref, bf16[8,1024,512]{2,1,0:T(8,128)(2,1)} %all-to-all-done.q_ref, bf16[8,1,1024,256]{3,2,1,0:T(8,128)(2,1)} %bitcast.5.k_ref.v_ref, bf16[8,1,1024,256]{3,2,1,0:T(8,128)(2,1)} %bitcast.5.k_ref.v_ref), custom_call_target="tpu_custom_call" | custom-call | flops 42949672960 | bytes 20971520 | tf_op jit(solution)/shard_map/attention/pallas_call | solution.py:240
  693.7 34.4 %attention.7.o_ref = bf16[8,1024,512]{2,1,0:T(8,128)(2,1)} custom-call(s32[1]{0:T(128)} %bitcast.idx_ref, bf16[8,1024,512]{2,1,0:T(8,128)(2,1)} %q_project.7.q_ref, bf16[8,8,1024,256]{3,2,1,0:T(8,128)(2,1)} %bitcast.47, bf16[8,8,1024,256]{3,2,1,0:T(8,128)(2,1)} %bitcast.48), custom_call_target="tpu_custom_call" | custom-call | flops 68719476736 | bytes 50331648 | tf_op jit(solution)/shard_map/attention/pallas_call | solution.py:240
  728.1 34.4 %attention.6.o_ref = bf16[8,1024,512]{2,1,0:T(8,128)(2,1)} custom-call(s32[1]{0:T(128)} %bitcast.idx_ref, bf16[8,1024,512]{2,1,0:T(8,128)(2,1)} %q_project.6.q_ref, bf16[8,8,1024,256]{3,2,1,0:T(8,128)(2,1)} %bitcast.49, bf16[8,8,1024,256]{3,2,1,0:T(8,128)(2,1)} %bitcast.50), custom_call_target="tpu_custom_call" | custom-call | flops 68719476736 | bytes 50331648 | tf_op jit(solution)/shard_map/attention/pallas_call | solution.py:240
  762.5 154.0 %all-to-all-start.2 = ((bf16[8,1024,512]{2,1,0:T(8,128)(2,1)}), bf16[8,1024,512]{2,1,0:T(8,128)(2,1)}, u32[]{:S(2)}, u32[]{:S(2)}) async-start(bf16[8,1024,512]{2,1,0:T(8,128)(2,1)} %attention.4), calls=%async_computation.2 | async-start | bytes 16777216 | tf_op jit(solution)/shard_map/all_to_all | solution.py:271
  916.5 43.8 %out_project.4.rest_0_ = bf16[4096,4096]{1,0:T(8,128)(2,1)} custom-call(bf16[8,1024,512]{2,1,0:T(8,128)(2,1)} %attention.7.o_ref, bf16[4096,4096]{1,0:T(8,128)(2,1)} %w_ref.15, bf16[4096,4096]{1,0:T(8,128)(2,1)} %bitcast.36), custom_call_target="tpu_custom_call" | custom-call | flops 34359738368 | bytes 58720256 | tf_op jit(solution)/shard_map/out_project/pallas_call | solution.py:140
  960.3 43.8 %out_project.5.rest_0_ = bf16[4096,4096]{1,0:T(8,128)(2,1)} custom-call(bf16[8,1024,512]{2,1,0:T(8,128)(2,1)} %attention.6.o_ref, bf16[4096,4096]{1,0:T(8,128)(2,1)} %w_ref.15, bf16[4096,4096]{1,0:T(8,128)(2,1)} %bitcast.37, bf16[4096,4096]{1,0:T(8,128)(2,1)} %out_project.4.rest_0_), custom_call_target="tpu_custom_call", output_to_operand_aliasing={{}: (3, {})} | custom-call | flops 34359738368 | bytes 58720256 | tf_op jit(solution)/shard_map/out_project/pallas_call | solution.py:140
  1004.0 43.8 %out_project.6.rest_0_ = bf16[4096,4096]{1,0:T(8,128)(2,1)} custom-call(bf16[8,1024,512]{2,1,0:T(8,128)(2,1)} %all-to-all-done.5.o_ref, bf16[4096,4096]{1,0:T(8,128)(2,1)} %w_ref.15, bf16[4096,4096]{1,0:T(8,128)(2,1)} %bitcast.38, bf16[4096,4096]{1,0:T(8,128)(2,1)} %out_project.5.rest_0_), custom_call_target="tpu_custom_call", output_to_operand_aliasing={{}: (3, {})} | custom-call | flops 34359738368 | bytes 58720256 | tf_op jit(solution)/shard_map/out_project/pallas_call | solution.py:140
  1047.8 43.8 %out_project.7 = bf16[4096,4096]{1,0:T(8,128)(2,1)} custom-call(bf16[8,1024,512]{2,1,0:T(8,128)(2,1)} %all-to-all-done.2.o_ref, bf16[4096,4096]{1,0:T(8,128)(2,1)} %w_ref.15, bf16[4096,4096]{1,0:T(8,128)(2,1)} %bitcast.39, bf16[4096,4096]{1,0:T(8,128)(2,1)} %out_project.6.rest_0_), custom_call_target="tpu_custom_call", output_to_operand_aliasing={{}: (3, {})} | custom-call | flops 34359738368 | bytes 58720256 | tf_op jit(solution)/shard_map/out_project/pallas_call | solution.py:140
  (27 shorter events, 12.2 us)
Async XLA Ops:
  7.2 686.5 %all-gather.7.cloned.1.call-start = ((), (), s32[]{:S(2)}) async-start(), calls=%async_computation.7 | async-start | bytes 37748736 | tf_op jit(solution)/shard_map/all_gather | solution.py:280
  39.9 688.2 %all-gather.5.cloned.1.call-start = ((), (), s32[]{:S(2)}) async-start(), calls=%async_computation.6 | async-start | bytes 37748736 | tf_op jit(solution)/shard_map/all_gather | solution.py:280
  97.8 98.9 %all-to-all-start.4 = ((bf16[8,1024,256]{2,1,0:T(8,128)(2,1)}), bf16[8,1024,256]{2,1,0:T(8,128)(2,1)}, u32[]{:S(2)}, u32[]{:S(2)}) async-start(bf16[8,1024,256]{2,1,0:T(8,128)(2,1)} %get-tuple-element.14), calls=%async_computation.4 | async-start | bytes 8388608 | tf_op jit(solution)/shard_map/all_to_all | solution.py:271
  102.4 4.1 copy-start
  138.2 62.2 %copy-start.4 = (bf16[128]{0:T(256)(128)(2,1)S(1)}, bf16[128]{0:T(256)(128)(2,1)}, u32[]{:S(2)}) copy-start(bf16[128]{0:T(256)(128)(2,1)} %param.14) | copy-start | bytes 772
  196.7 88.8 %all-to-all-start.1 = ((bf16[8,1024,256]{2,1,0:T(8,128)(2,1)}), bf16[8,1024,256]{2,1,0:T(8,128)(2,1)}, u32[]{:S(2)}, u32[]{:S(2)}) async-start(bf16[8,1024,256]{2,1,0:T(8,128)(2,1)} %get-tuple-element.12), calls=%async_computation.1 | async-start | bytes 8388608 | tf_op jit(solution)/shard_map/all_to_all | solution.py:271
  285.5 142.8 %all-to-all-start.3 = ((bf16[8,1024,512]{2,1,0:T(8,128)(2,1)}), bf16[8,1024,512]{2,1,0:T(8,128)(2,1)}, u32[]{:S(2)}, u32[]{:S(2)}) async-start(bf16[8,1024,512]{2,1,0:T(8,128)(2,1)} %q_project.5), calls=%async_computation.3 | async-start | bytes 16777216 | tf_op jit(solution)/shard_map/all_to_all | solution.py:271
  289.4 4.1 copy-start.1
  289.4 4.1 copy-start.2
  289.4 4.9 copy-start.3
  428.2 184.0 %all-to-all-start = ((bf16[8,1024,512]{2,1,0:T(8,128)(2,1)}), bf16[8,1024,512]{2,1,0:T(8,128)(2,1)}, u32[]{:S(2)}, u32[]{:S(2)}) async-start(bf16[8,1024,512]{2,1,0:T(8,128)(2,1)} %q_project.4), calls=%async_computation | async-start | bytes 16777216 | tf_op jit(solution)/shard_map/all_to_all | solution.py:271
  612.2 150.3 %all-to-all-start.5 = ((bf16[8,1024,512]{2,1,0:T(8,128)(2,1)}), bf16[8,1024,512]{2,1,0:T(8,128)(2,1)}, u32[]{:S(2)}, u32[]{:S(2)}) async-start(bf16[8,1024,512]{2,1,0:T(8,128)(2,1)} %attention.5), calls=%async_computation.5 | async-start | bytes 16777216 | tf_op jit(solution)/shard_map/all_to_all | solution.py:271
  762.5 285.3 %all-to-all-start.2 = ((bf16[8,1024,512]{2,1,0:T(8,128)(2,1)}), bf16[8,1024,512]{2,1,0:T(8,128)(2,1)}, u32[]{:S(2)}, u32[]{:S(2)}) async-start(bf16[8,1024,512]{2,1,0:T(8,128)(2,1)} %attention.4), calls=%async_computation.2 | async-start | bytes 16777216 | tf_op jit(solution)/shard_map/all_to_all | solution.py:271
Sparse Core Ops, SparseCore 0:
  40.0 238.0 all-gather.6
  279.9 330.4 all-gather.4
